TPU v7x, 32 devices: a whole 2x2x4 slice. The times are simulated.
32 devices in a mesh: dp: 8 (over z, y), tp: 4 (over x, core).
Axes of the slice: x: 2, y: 2, z: 4, core: 2. Of those that a mesh axis runs over, the one named last changes fastest.
Arguments:
- x_teach: bfloat16 [64, 256, 1024], P('dp', 'tp')
- x_stud: bfloat16 [64, 256, 312], P(('dp', 'tp'))
- w_up_t: bfloat16 [8, 1024, 4096], P(None, None, 'tp')
- w_down_t: bfloat16 [8, 4096, 1024], P(None, 'tp')
- gain_t: float32 [8, 1024], replicated
- head_t: bfloat16 [1024, 30592], P(None, 'tp')
- w_up_s: bfloat16 [2, 312, 1248], replicated
- w_down_s: bfloat16 [2, 1248, 312], replicated
- gain_s: float32 [2, 312], replicated
- proj_s: bfloat16 [2, 312, 1024], replicated
- head_s: bfloat16 [312, 30592], replicated
Outputs:
- output 1: float32 [], replicated
- output 2: float32 [2, 312, 1248], replicated
- output 3: float32 [2, 1248, 312], replicated
- output 4: float32 [2, 312], replicated
- output 5: float32 [2, 312, 1024], replicated
- output 6: float32 [312, 30592], replicated
All inputs are finite; a program needn't handle non-finite values.
Results may differ from a plain program's by a relative error of at most 0.00335172.
Values are sent between devices in bfloat16 or wider.
A program may use at most 1 GiB of HBM per device.

v0:
```python
import jax
import jax.numpy as jnp
from jax import lax
from jax.sharding import PartitionSpec as P

NORM_EPS = 1e-6


def rms_parts(values):
    vals32 = values.astype(jnp.float32)
    inv_rms = lax.rsqrt(jnp.mean(vals32 * vals32, axis=-1, keepdims=True) + NORM_EPS)
    return vals32 * inv_rms, inv_rms


def rms_back(normed, inv_rms, grad_out):
    return inv_rms * (grad_out - normed * jnp.mean(grad_out * normed, axis=-1, keepdims=True))


def gelu_tanh(values):
    return jax.nn.gelu(values, approximate=True)


def gelu_back(pre_act, grad_out):
    return jax.vjp(gelu_tanh, pre_act)[1](grad_out)[0]


def mat_mul(subscripts, lhs_arr, rhs_arr):
    return jnp.einsum(subscripts, lhs_arr, rhs_arr, preferred_element_type=jnp.float32)


def student_forward(x_stud, w_up_s, w_down_s, gain_s, proj_s, features):
    residual = x_stud.astype(jnp.float32)
    norm_cur, inv_cur = rms_parts(residual)
    saved_acts = []
    err_total = jnp.zeros((), jnp.float32)
    for layer_idx in range(w_up_s.shape[0]):
        normed = (norm_cur * gain_s[layer_idx]).astype(jnp.bfloat16)
        pre_act = mat_mul('bsd,df->bsf', normed, w_up_s[layer_idx])
        hidden_act = gelu_tanh(pre_act).astype(jnp.bfloat16)
        residual = residual + mat_mul('bsf,fd->bsd', hidden_act, w_down_s[layer_idx])
        norm_next, inv_next = rms_parts(residual)
        proj_in = norm_next.astype(jnp.bfloat16)
        feat_err = mat_mul('bsd,de->bse', proj_in, proj_s[layer_idx]) - features[layer_idx]
        err_total = err_total + jnp.sum(feat_err * feat_err)
        saved_acts.append((norm_cur, inv_cur, normed, pre_act, hidden_act, norm_next, inv_next, proj_in, feat_err))
        norm_cur, inv_cur = norm_next, inv_next
    return saved_acts, err_total


def student_backward(saved_acts, w_up_s, w_down_s, gain_s, proj_s, feat_coef, head_in_grad):
    n_layers = len(saved_acts)
    up_grads = []
    down_grads = []
    gain_grads = []
    proj_grads = []
    resid_grad = None
    for layer_idx in reversed(range(n_layers)):
        norm_cur, inv_cur, normed, pre_act, hidden_act, norm_next, inv_next, proj_in, feat_err = saved_acts[layer_idx]
        err_grad = (2.0 * feat_coef * feat_err).astype(jnp.bfloat16)
        proj_grads.append(mat_mul('bsd,bse->de', proj_in, err_grad))
        out_grad = mat_mul('bse,de->bsd', err_grad, proj_s[layer_idx])
        if resid_grad is None:
            resid_grad = rms_back(norm_next, inv_next, out_grad + head_in_grad)
        else:
            resid_grad = resid_grad + rms_back(norm_next, inv_next, out_grad)
        resid_bf = resid_grad.astype(jnp.bfloat16)
        down_grads.append(mat_mul('bsf,bsd->fd', hidden_act, resid_bf))
        act_grad = mat_mul('bsd,fd->bsf', resid_bf, w_down_s[layer_idx])
        pre_grad = gelu_back(pre_act, act_grad).astype(jnp.bfloat16)
        up_grads.append(mat_mul('bsd,bsf->df', normed, pre_grad))
        norm_grad = mat_mul('bsf,df->bsd', pre_grad, w_up_s[layer_idx])
        gain_grads.append(jnp.sum(norm_grad * norm_cur, axis=(0, 1)))
        if layer_idx > 0:
            resid_grad = resid_grad + rms_back(norm_cur, inv_cur, norm_grad * gain_s[layer_idx])
    return (jnp.stack(up_grads[::-1]), jnp.stack(down_grads[::-1]),
            jnp.stack(gain_grads[::-1]), jnp.stack(proj_grads[::-1]))


def solution(mesh):
    dp_size = mesh.shape['dp']
    tp_size = mesh.shape['tp']

    def local_step(x_teach, x_stud, w_up_t, w_down_t, gain_t, head_t, w_up_s, w_down_s, gain_s, proj_s, head_s):
        n_feat = w_up_s.shape[0]
        per_feat = w_up_t.shape[0] // n_feat
        hidden = x_teach
        features = []
        for layer_idx in range(w_up_t.shape[0]):
            normed = (rms_parts(hidden)[0] * gain_t[layer_idx]).astype(jnp.bfloat16)
            gathered = lax.all_gather(normed, 'tp', axis=1, tiled=True)
            hidden_act = gelu_tanh(mat_mul('bsd,df->bsf', gathered, w_up_t[layer_idx])).astype(jnp.bfloat16)
            partial_out = mat_mul('bsf,fd->bsd', hidden_act, w_down_t[layer_idx])
            layer_out = lax.psum_scatter(partial_out, 'tp', scatter_dimension=1, tiled=True)
            hidden = hidden + layer_out.astype(jnp.bfloat16)
            if (layer_idx + 1) % per_feat == 0:
                features.append(lax.all_to_all(hidden, 'tp', 0, 1, tiled=True))
        final_norm = rms_parts(hidden)[0].astype(jnp.bfloat16)
        final_full = lax.all_gather(final_norm, 'tp', axis=1, tiled=True)
        teach_logits = mat_mul('bsd,dv->bsv', final_full, head_t)

        n_tokens = x_stud.shape[0] * x_stud.shape[1] * dp_size * tp_size
        feat_coef = 1.0 / (n_feat * n_tokens * head_t.shape[0])
        kl_coef = 1.0 / n_tokens
        saved_acts, err_total = student_forward(x_stud, w_up_s, w_down_s, gain_s, proj_s, features)
        head_in = saved_acts[-1][7]
        stud_full = lax.all_gather(head_in, 'tp', axis=0, tiled=True)
        vocab_part = head_t.shape[1]
        head_cols = lax.dynamic_slice_in_dim(head_s, lax.axis_index('tp') * vocab_part, vocab_part, axis=1)
        stud_logits = mat_mul('bsd,dv->bsv', stud_full, head_cols)
        peak_vals = lax.pmax(jnp.stack([jnp.max(teach_logits, axis=-1), jnp.max(stud_logits, axis=-1)]), 'tp')
        teach_exp = jnp.exp(teach_logits - peak_vals[0][..., None])
        stud_exp = jnp.exp(stud_logits - peak_vals[1][..., None])
        sum_vals = lax.psum(jnp.stack([jnp.sum(teach_exp, axis=-1), jnp.sum(stud_exp, axis=-1)]), 'tp')
        log_norms = peak_vals + jnp.log(sum_vals)
        teach_prob = teach_exp / sum_vals[0][..., None]
        stud_prob = stud_exp / sum_vals[1][..., None]
        log_ratio = teach_logits - stud_logits - (log_norms[0] - log_norms[1])[..., None]
        kl_local = jnp.sum(teach_prob * log_ratio)
        logit_grad = (kl_coef * (stud_prob - teach_prob)).astype(jnp.bfloat16)
        head_part = mat_mul('bsd,bsv->dv', stud_full, logit_grad)
        head_grad = lax.all_gather(lax.psum(head_part, 'dp'), 'tp', axis=1, tiled=True)
        full_in_grad = mat_mul('bsv,dv->bsd', logit_grad, head_cols)
        head_in_grad = lax.psum_scatter(full_in_grad, 'tp', scatter_dimension=0, tiled=True)
        local_grads = student_backward(saved_acts, w_up_s, w_down_s, gain_s, proj_s, feat_coef, head_in_grad)
        grad_up, grad_down, grad_gain, grad_proj = lax.psum(local_grads, ('dp', 'tp'))
        total_loss = lax.psum(feat_coef * err_total + kl_coef * kl_local, ('dp', 'tp'))
        return total_loss, grad_up, grad_down, grad_gain, grad_proj, head_grad

    in_specs = (P('dp', 'tp', None), P(('dp', 'tp'), None, None), P(None, None, 'tp'), P(None, 'tp', None),
                P(), P(None, 'tp'), P(), P(), P(), P(), P())
    out_specs = (P(), P(), P(), P(), P(), P())
    return jax.shard_map(local_step, mesh=mesh, in_specs=in_specs, out_specs=out_specs, check_vma=False)
```

profile of v0, /device:TPU:0, one launch (start us, length us, event | category | flops | bytes accessed | tf_op | source)
XLA Modules:
  0.0 2010.3 jit_solution(7384957400305055916)
XLA Ops:
  13.0 37.1 %all-gather.13.cloned.1.call-done = bf16[8,256,1024]{2,1,0:T(8,128)(2,1)} async-done(((bf16[8,64,1024]{2,1,0:T(8,128)(2,1)}), bf16[8,256,1024]{2,1,0:T(8,128)(2,1)}) %all-gather.13.cloned.1.call-update) | async-done | bytes 4194320 | tf_op jit(solution)/shard_map/all_gather | solution.py:90
  64.2 70.7 %reduce-scatter.10.cloned.1.call-done = f32[8,64,1024]{2,1,0:T(8,128)} async-done(((f32[8,256,1024]{2,1,0:T(8,128)}), f32[8,64,1024]{2,1,0:T(8,128)}) %reduce-scatter.10.cloned.1.call-update) | async-done | bytes 2097168 | tf_op jit(solution)/shard_map/reduce_scatter | solution.py:93
  138.3 34.4 %all-gather.15.cloned.1.call-done = bf16[8,256,1024]{2,1,0:T(8,128)(2,1)} async-done(((bf16[8,64,1024]{2,1,0:T(8,128)(2,1)}), bf16[8,256,1024]{2,1,0:T(8,128)(2,1)}) %all-gather.15.cloned.1.call-update) | async-done | bytes 4194320 | tf_op jit(solution)/shard_map/all_gather | solution.py:90
  186.9 70.7 %reduce-scatter.12.cloned.1.call-done = f32[8,64,1024]{2,1,0:T(8,128)} async-done(((f32[8,256,1024]{2,1,0:T(8,128)}), f32[8,64,1024]{2,1,0:T(8,128)}) %reduce-scatter.12.cloned.1.call-update) | async-done | bytes 2097168 | tf_op jit(solution)/shard_map/reduce_scatter | solution.py:93
  309.5 70.7 %reduce-scatter.14.cloned.1.call-done = f32[8,64,1024]{2,1,0:T(8,128)} async-done(((f32[8,256,1024]{2,1,0:T(8,128)}), f32[8,64,1024]{2,1,0:T(8,128)}) %reduce-scatter.14.cloned.1.call-update) | async-done | bytes 2097168 | tf_op jit(solution)/shard_map/reduce_scatter | solution.py:93
  383.5 34.4 %all-gather.19.cloned.1.call-done = bf16[8,256,1024]{2,1,0:T(8,128)(2,1)} async-done(((bf16[8,64,1024]{2,1,0:T(8,128)(2,1)}), bf16[8,256,1024]{2,1,0:T(8,128)(2,1)}) %all-gather.19.cloned.1.call-update) | async-done | bytes 4194320 | tf_op jit(solution)/shard_map/all_gather | solution.py:90
  432.1 70.7 %reduce-scatter.16.cloned.1.call-done = f32[8,64,1024]{2,1,0:T(8,128)} async-done(((f32[8,256,1024]{2,1,0:T(8,128)}), f32[8,64,1024]{2,1,0:T(8,128)}) %reduce-scatter.16.cloned.1.call-update) | async-done | bytes 2097168 | tf_op jit(solution)/shard_map/reduce_scatter | solution.py:93
  506.2 34.4 %all-gather.21.cloned.1.call-done = bf16[8,256,1024]{2,1,0:T(8,128)(2,1)} async-done(((bf16[8,64,1024]{2,1,0:T(8,128)(2,1)}), bf16[8,256,1024]{2,1,0:T(8,128)(2,1)}) %all-gather.21.cloned.1.call-update) | async-done | bytes 4194320 | tf_op jit(solution)/shard_map/all_gather | solution.py:90
  554.9 70.6 %reduce-scatter.18.cloned.1.call-done = f32[8,64,1024]{2,1,0:T(8,128)} async-done(((f32[8,256,1024]{2,1,0:T(8,128)}), f32[8,64,1024]{2,1,0:T(8,128)}) %reduce-scatter.18.cloned.1.call-update) | async-done | bytes 2097168 | tf_op jit(solution)/shard_map/reduce_scatter | solution.py:93
  628.8 34.4 %all-gather.23.cloned.1.call-done = bf16[8,256,1024]{2,1,0:T(8,128)(2,1)} async-done(((bf16[8,64,1024]{2,1,0:T(8,128)(2,1)}), bf16[8,256,1024]{2,1,0:T(8,128)(2,1)}) %all-gather.23.cloned.1.call-update) | async-done | bytes 4194320 | tf_op jit(solution)/shard_map/all_gather | solution.py:90
  677.3 70.7 %reduce-scatter.20.cloned.1.call-done = f32[8,64,1024]{2,1,0:T(8,128)} async-done(((f32[8,256,1024]{2,1,0:T(8,128)}), f32[8,64,1024]{2,1,0:T(8,128)}) %reduce-scatter.20.cloned.1.call-update) | async-done | bytes 2097168 | tf_op jit(solution)/shard_map/reduce_scatter | solution.py:93
  751.4 34.4 %all-gather.25.cloned.1.call-done = bf16[8,256,1024]{2,1,0:T(8,128)(2,1)} async-done(((bf16[8,64,1024]{2,1,0:T(8,128)(2,1)}), bf16[8,256,1024]{2,1,0:T(8,128)(2,1)}) %all-gather.25.cloned.1.call-update) | async-done | bytes 4194320 | tf_op jit(solution)/shard_map/all_gather | solution.py:90
  799.9 70.7 %reduce-scatter.22.cloned.1.call-done = f32[8,64,1024]{2,1,0:T(8,128)} async-done(((f32[8,256,1024]{2,1,0:T(8,128)}), f32[8,64,1024]{2,1,0:T(8,128)}) %reduce-scatter.22.cloned.1.call-update) | async-done | bytes 2097168 | tf_op jit(solution)/shard_map/reduce_scatter | solution.py:93
  874.2 34.2 %all-gather.27.cloned.1.call-done = bf16[8,256,1024]{2,1,0:T(8,128)(2,1)} async-done(((bf16[8,64,1024]{2,1,0:T(8,128)(2,1)}), bf16[8,256,1024]{2,1,0:T(8,128)(2,1)}) %all-gather.27.cloned.1.call-update) | async-done | bytes 4194320 | tf_op jit(solution)/shard_map/all_gather | solution.py:90
  930.5 62.8 %reduce-scatter.24.cloned.1.call-done = f32[8,64,1024]{2,1,0:T(8,128)} async-done(((f32[8,256,1024]{2,1,0:T(8,128)}), f32[8,64,1024]{2,1,0:T(8,128)}) %reduce-scatter.24.cloned.1.call-update) | async-done | bytes 2097168 | tf_op jit(solution)/shard_map/reduce_scatter | solution.py:93
  1048.8 41.0 %fusion.311 = (f32[8,256]{1,0:T(8,128)S(1)}, f32[8,256,7648]{1,2,0:T(8,128)}) fusion(bf16[8,256,1024]{2,1,0:T(8,128)(2,1)} %all-gather.29.cloned.1.call-done, bf16[1024,7648]{0,1:T(8,128)(2,1)} %param.16), kind=kOutput, calls=%fused_computation.372 | convolution fusion | flops 32093698048 | bytes 82518016 | tf_op jit(solution)/shard_map/bsd,dv->bsv/dot_general | solution.py:28
  1100.0 38.8 %fusion.1 = (f32[8,256]{1,0:T(8,128)S(1)}, f32[8,256]{1,0:T(8,128)S(1)}) fusion(f32[8,256,7648]{1,2,0:T(8,128)} %get-tuple-element.57, f32[8,256]{1,0:T(8,128)S(1)} %get-tuple-element.44, f32[8,256,7648]{1,2,0:T(8,128)} %get-tuple-element.55, f32[8,256]{1,0:T(8,128)S(1)} %get-tuple-element.45), kind=kLoop, calls=%fused_computation.5 | loop fusion | flops 62648320 | bytes 125337600 | tf_op jit(solution)/shard_map/reduce_sum | solution.py:113
  1149.1 50.9 %multiply_convert_fusion = (bf16[8,256,7648]{1,2,0:T(8,128)(2,1)}, f32[]{:T(128)}) fusion(f32[8,256,7648]{1,2,0:T(8,128)} %get-tuple-element.55, f32[8,256,7648]{1,2,0:T(8,128)} %get-tuple-element.57, f32[8,256]{1,0:T(8,128)S(1)} %get-tuple-element.42, f32[8,256]{1,0:T(8,128)S(1)} %get-tuple-element.43, f32[8,256]{1,0:T(8,128)S(1)} %get-tuple-element.45, ...), kind=kLoop, calls=%fused_computation | loop fusion | flops 172294144 | bytes 156672000 | tf_op jit(solution)/shard_map/convert_element_type | solution.py:119
  1236.9 283.8 %all-reduce.5.cloned.1.call-done = f32[312,7648]{1,0:T(8,128)} async-done(((f32[312,7648]{1,0:T(8,128)}), f32[312,7648]{1,0:T(8,128)}) %all-reduce.5.cloned.1.call-update) | async-done | bytes 9544720 | tf_op jit(solution)/shard_map/psum | solution.py:121
  1593.0 40.0 %all-reduce = (f32[]{:T(128)}, f32[2,312]{1,0:T(2,128)}) all-reduce(f32[]{:T(128)S(6)} %add.290, f32[2,312]{1,0:T(2,128)S(1)} %pad_maximum_fusion.5), channel_id=1, replica_groups=mesh['dp'=8,'tp'=4] {'dp','tp'}, use_global_device_ids=true, to_apply=%region_29.0 | all-reduce | flops 625 | bytes 5000 | tf_op jit(solution)/shard_map/psum | solution.py:126
  1633.0 168.7 %all-gather.33.cloned.1.call-done = f32[4,7648,312]{1,2,0:T(8,128)} async-done(((f32[1,7648,312]{1,2,0:T(8,128)}), f32[4,7648,312]{1,2,0:T(8,128)}) %all-gather.33.cloned.1.call-update) | async-done | bytes 38178832 | tf_op jit(solution)/shard_map/all_gather | solution.py:121
  1801.7 41.3 %copy.24 = f32[4,7648,312]{1,0,2:T(4,128)} copy(f32[4,7648,312]{1,2,0:T(8,128)} %all-gather.33.cloned.1.call-done) | data formatting | bytes 76357632 | tf_op jit(solution)/shard_map/all_gather | solution.py:121
  1843.0 44.2 %reshape.157 = f32[30592,312]{0,1:T(8,128)} reshape(f32[4,7648,312]{1,0,2:T(4,128)} %copy.24) | data formatting | bytes 76357632
  1887.3 107.5 %all-reduce.7.cloned.1.call-done = (f32[2,312,1248]{2,1,0:T(8,128)}, f32[2,1248,312]{1,2,0:T(8,128)}, f32[2,312,1024]{2,1,0:T(8,128)}) async-done(((f32[2,312,1248]{2,1,0:T(8,128)}, f32[2,1248,312]{1,2,0:T(8,128)}, f32[2,312,1024]{2,1,0:T(8,128)}), (f32[2,312,1248]{2,1,0:T(8,128)}, f32[2,1248,312]{1,2,0:T(8,128)}, f32[2,312,1024]{2,1,0:T(8,128)})) %all-reduce.7.cloned.1.call-update) | async-done | bytes 8785936 | tf_op jit(solution)/shard_map/psum | solution.py:125
  (216 shorter events, 375.7 us)
Async XLA Ops:
  7.2 43.0 %all-gather.13.cloned.1.call-start = ((), (), s32[]{:S(2)}) async-start(), calls=%async_computation.11 | async-start | bytes 5242880 | tf_op jit(solution)/shard_map/all_gather | solution.py:90
  12.9 122.1 %reduce-scatter.10.cloned.1.call-start = ((), (), s32[]{:S(2)}) async-start(), calls=%async_computation.12 | async-start | bytes 10485760 | tf_op jit(solution)/shard_map/reduce_scatter | solution.py:93
  64.2 108.5 %all-gather.15.cloned.1.call-start = ((), (), s32[]{:S(2)}) async-start(), calls=%async_computation.13 | async-start | bytes 5242880 | tf_op jit(solution)/shard_map/all_gather | solution.py:90
  138.3 119.3 %reduce-scatter.12.cloned.1.call-start = ((), (), s32[]{:S(2)}) async-start(), calls=%async_computation.14 | async-start | bytes 10485760 | tf_op jit(solution)/shard_map/reduce_scatter | solution.py:93
  186.8 108.5 %all-gather.17.cloned.1.call-start = ((), (), s32[]{:S(2)}) async-start(), calls=%async_computation.15 | async-start | bytes 5242880 | tf_op jit(solution)/shard_map/all_gather | solution.py:90
  260.9 119.3 %reduce-scatter.14.cloned.1.call-start = ((), (), s32[]{:S(2)}) async-start(), calls=%async_computation.16 | async-start | bytes 10485760 | tf_op jit(solution)/shard_map/reduce_scatter | solution.py:93
  309.4 108.5 %all-gather.19.cloned.1.call-start = ((), (), s32[]{:S(2)}) async-start(), calls=%async_computation.17 | async-start | bytes 5242880 | tf_op jit(solution)/shard_map/all_gather | solution.py:90
  383.5 119.3 %reduce-scatter.16.cloned.1.call-start = ((), (), s32[]{:S(2)}) async-start(), calls=%async_computation.18 | async-start | bytes 10485760 | tf_op jit(solution)/shard_map/reduce_scatter | solution.py:93
  432.0 108.5 %all-gather.21.cloned.1.call-start = ((), (), s32[]{:S(2)}) async-start(), calls=%async_computation.19 | async-start | bytes 5242880 | tf_op jit(solution)/shard_map/all_gather | solution.py:90
  504.8 120.7 %copy-start = (bf16[8,64,1024]{2,1,0:T(8,128)(2,1)}, bf16[8,64,1024]{2,1,0:T(8,128)(2,1)S(1)}, u32[]{:S(2)}) copy-start(bf16[8,64,1024]{2,1,0:T(8,128)(2,1)S(1)} %get-tuple-element.25) | copy-start | bytes 3145732
  506.1 119.3 %reduce-scatter.18.cloned.1.call-start = ((), (), s32[]{:S(2)}) async-start(), calls=%async_computation.20 | async-start | bytes 10485760 | tf_op jit(solution)/shard_map/reduce_scatter | solution.py:93
  554.6 108.5 %all-gather.23.cloned.1.call-start = ((), (), s32[]{:S(2)}) async-start(), calls=%async_computation.21 | async-start | bytes 5242880 | tf_op jit(solution)/shard_map/all_gather | solution.py:90
  628.7 119.3 %reduce-scatter.20.cloned.1.call-start = ((), (), s32[]{:S(2)}) async-start(), calls=%async_computation.22 | async-start | bytes 10485760 | tf_op jit(solution)/shard_map/reduce_scatter | solution.py:93
  677.3 108.5 %all-gather.25.cloned.1.call-start = ((), (), s32[]{:S(2)}) async-start(), calls=%async_computation.23 | async-start | bytes 5242880 | tf_op jit(solution)/shard_map/all_gather | solution.py:90
  751.3 119.3 %reduce-scatter.22.cloned.1.call-start = ((), (), s32[]{:S(2)}) async-start(), calls=%async_computation.24 | async-start | bytes 10485760 | tf_op jit(solution)/shard_map/reduce_scatter | solution.py:93
  799.9 108.5 %all-gather.27.cloned.1.call-start = ((), (), s32[]{:S(2)}) async-start(), calls=%async_computation.25 | async-start | bytes 5242880 | tf_op jit(solution)/shard_map/all_gather | solution.py:90
  873.9 119.3 %reduce-scatter.24.cloned.1.call-start = ((), (), s32[]{:S(2)}) async-start(), calls=%async_computation.26 | async-start | bytes 10485760 | tf_op jit(solution)/shard_map/reduce_scatter | solution.py:93
  922.5 90.0 %all-gather.31.cloned.1.call-start = ((), (), s32[]{:S(2)}) async-start(), calls=%async_computation.28 | async-start | bytes 1597440 | tf_op jit(solution)/shard_map/all_gather | solution.py:106
  930.5 118.3 %all-gather.29.cloned.1.call-start = ((), (), s32[]{:S(2)}) async-start(), calls=%async_computation.27 | async-start | bytes 5242880 | tf_op jit(solution)/shard_map/all_gather | solution.py:98
  998.6 522.1 %all-reduce.5.cloned.1.call-start = ((), (), s32[]{:S(2)}) async-start(), calls=%async_computation.30 | async-start | bytes 19169280 | tf_op jit(solution)/shard_map/psum | solution.py:121
  1218.5 354.4 %reduce-scatter.26.cloned.1.call-start = ((), (), s32[]{:S(2)}) async-start(), calls=%async_computation.29 | async-start | bytes 3194880 | tf_op jit(solution)/shard_map/reduce_scatter | solution.py:123
  1236.8 564.9 %all-gather.33.cloned.1.call-start = ((), (), s32[]{:S(2)}) async-start(), calls=%async_computation.31 | async-start | bytes 47923200 | tf_op jit(solution)/shard_map/all_gather | solution.py:121
  1539.1 27.5 %all-to-all-start.1 = ((bf16[8,64,1024]{2,1,0:T(8,128)(2,1)}), bf16[8,64,1024]{2,1,0:T(8,128)(2,1)}, u32[]{:S(2)}, u32[]{:S(2)}) async-start(bf16[8,64,1024]{2,1,0:T(8,128)(2,1)} %get-tuple-element.17), calls=%async_computation.9 | async-start | bytes 2097152 | tf_op jit(solution)/shard_map/all_to_all | solution.py:96
  1543.4 451.4 %all-reduce.7.cloned.1.call-start = ((), (), s32[]{:S(2)}) async-start(), calls=%async_computation.32 | async-start | bytes 17891328 | tf_op jit(solution)/shard_map/psum | solution.py:125
  (38 other events, 285.3 us)
Sparse Core Ops, SparseCore 0:
  13.0 37.0 all-gather.12
  64.3 70.6 reduce-scatter.9
  138.4 34.2 all-gather.14
  186.9 70.6 reduce-scatter.11
  261.0 34.2 all-gather.16
  309.5 70.6 reduce-scatter.13
  383.6 34.2 all-gather.18
  432.1 70.6 reduce-scatter.15
  506.2 34.2 all-gather.20
  554.8 70.6 reduce-scatter.17
  628.9 34.2 all-gather.22
  677.4 70.6 reduce-scatter.19
  751.5 34.2 all-gather.24
  800.0 70.6 reduce-scatter.21
  874.1 34.2 all-gather.26
  922.6 70.6 reduce-scatter.23
  994.7 17.7 all-gather.30
  1014.5 34.2 all-gather.28
  1218.6 302.0 all-reduce.4
  1523.7 42.2 reduce-scatter.25
  1567.6 234.0 all-gather.32
  1808.6 186.1 all-reduce.6
where the time goes:
time: 2020 us; the launch traced here: 2010 us
  waiting for transfers between devices  1430 us (71%)
  matrix products  242 us (12%)
  other arithmetic  129 us (6%)
  local copies, waits for them, and re-layouts  104 us (5%)
  blocking collectives  77.4 us (4%)
    reduce_scatter x8, waiting for transfers between devices, local_step(): lax.psum_scatter(partial_out, 'tp', scatter_dimension=1, tiled=True)  558 us
    psum x1, waiting for transfers between devices, local_step(): lax.psum(head_part, 'dp')  284 us
    all_gather x8, waiting for transfers between devices, local_step(): gathered = lax.all_gather(normed, 'tp', axis=1, tiled=True)  277 us
    dot_general x30, matrix products, mat_mul(): jnp.einsum(subscripts, lhs_arr, rhs_arr, preferred_element_type=jnp.float32)  242 us
    all_gather x1, waiting for transfers between devices, local_step(): lax.all_gather(lax.psum(head_part, 'dp'), 'tp', axis=1, tiled=True)  169 us
    psum x1, waiting for transfers between devices, local_step(): lax.psum(local_grads, ('dp', 'tp'))  108 us
    unnamed x82, local copies, waits for them, and re-layouts  59.3 us
    convert_element_type x1, other arithmetic, local_step(): logit_grad = (kl_coef * (stud_prob - teach_prob)).astype(jnp.bfloat16)  50.9 us
  transfers between devices with their start and end apart: 23, of which 22 were waited for; matrix products, arithmetic and copies ran while one was open for 8% of the time, Pallas kernels for 0%

commit v1 on v0

--- a/solution.py
+++ b/solution.py
@@ -1,6 +1,10 @@
+import functools
+
 import jax
 import jax.numpy as jnp
 from jax import lax
+from jax.experimental import pallas as pl
+from jax.experimental.pallas import tpu as pltpu
 from jax.sharding import PartitionSpec as P
 
 NORM_EPS = 1e-6
@@ -76,26 +80,260 @@
             jnp.stack(gain_grads[::-1]), jnp.stack(proj_grads[::-1]))
 
 
+MESH = pl.DeviceIdType.MESH
+N_DIRECT = 128
+N_SEED = 112
+
+
+def teacher_kernel(n_layers, x_ref, gain_ref, wu_ref, wd_ref, feat_ref, gu_ref, gd_ref,
+                   h_ref, n_ref, a_ref, acc_ref, wb_ref, load_sem, send_sem, recv_sem):
+    rows, d_model = x_ref.shape
+    width = wu_ref.shape[2]
+    per_feat = n_layers // feat_ref.shape[0]
+    own = (wu_ref, wd_ref)
+    got = (gu_ref, gd_ref)
+    n_dir, n_seed = direct_rows(d_model), seed_rows(d_model)
+    dp, tp = lax.axis_index('dp'), lax.axis_index('tp')
+    z, y = dp // 2, dp % 2
+    x, c = tp // 2, tp % 2
+    zz = z % 2
+    x_peer = (dp, (1 - x) * 2 + c)
+    y_peer = (z * 2 + 1 - y, tp)
+    z_peer = ((z + 1 - 2 * zz) * 2 + y, tp)
+    mate = (dp, x * 2 + 1 - c)
+    base_p, base_q = n_dir, n_dir + 4 * n_seed
+
+    def rows_p(yy, zb):
+        return pl.ds(pl.multiple_of(base_p + n_seed * (yy * 2 + zb), 16), n_seed)
+
+    def rows_q(yy, zb):
+        return pl.ds(pl.multiple_of(base_q + n_seed * (zb * 2 + yy), 16), n_seed)
+
+    def pair_p(yy):
+        return pl.ds(pl.multiple_of(base_p + 2 * n_seed * yy, 16), 2 * n_seed)
+
+    def pair_q(zb):
+        return pl.ds(pl.multiple_of(base_q + 2 * n_seed * zb, 16), 2 * n_seed)
+
+    def copy(stage, l, m, src, dst, dev):
+        t = 2 * l + m
+        return pltpu.make_async_remote_copy(src, dst, send_sem.at[stage, t], recv_sem.at[stage, t],
+                                            device_id=dev, device_id_type=MESH)
+
+    def outgoing(stage, l, m):
+        g, w = got[m], own[m]
+        if stage == 0:
+            r = rows_p(y, zz)
+            return copy(0, l, m, w.at[l, r], g.at[1, l, r], x_peer)
+        if stage == 1:
+            r = rows_q(y, zz)
+            return copy(1, l, m, w.at[l, r], g.at[1, l, r], x_peer)
+        if stage == 2:
+            r = pl.ds(0, n_dir)
+            return copy(2, l, m, w.at[l, r], g.at[1, l, r], x_peer)
+        if stage == 3:
+            r = rows_p(y, zz)
+            return copy(3, l, m, g.at[1, l, r], g.at[1, l, r], z_peer)
+        if stage == 4:
+            r = rows_q(y, zz)
+            return copy(4, l, m, g.at[1, l, r], g.at[1, l, r], y_peer)
+        if stage == 5:
+            r = pair_p(y)
+            return copy(5, l, m, g.at[1, l, r], g.at[1, l, r], y_peer)
+        if stage == 6:
+            r = pair_q(zz)
+            return copy(6, l, m, g.at[1, l, r], g.at[1, l, r], z_peer)
+        if stage == 7:
+            return copy(7, l, m, w.at[l], g.at[0, l], mate)
+        return copy(8, l, m, g.at[1, l], g.at[2, l], mate)
+
+    def incoming(stage, l, m):
+        g = got[m]
+        r = (rows_p(y, zz), rows_q(y, zz), pl.ds(0, n_dir), rows_p(y, 1 - zz), rows_q(1 - y, zz),
+             pair_p(1 - y), pair_q(1 - zz))
+        if stage < 7:
+            ref = g.at[1, l, r[stage]]
+        else:
+            ref = g.at[0, l] if stage == 7 else g.at[2, l]
+        return copy(stage, l, m, ref, ref, mate)
+
+    def send_x(l, m):
+        for stage in (0, 1, 2):
+            outgoing(stage, l, m).start()
+
+    def hop_a(l, m):
+        for stage, nxt in ((0, 3), (1, 4)):
+            incoming(stage, l, m).wait_recv()
+            outgoing(nxt, l, m).start()
+
+    def hop_b(l, m):
+        for stage, nxt in ((3, 5), (4, 6)):
+            incoming(stage, l, m).wait_recv()
+            outgoing(nxt, l, m).start()
+
+    def hop_c(l, m):
+        for stage in (2, 5, 6):
+            incoming(stage, l, m).wait_recv()
+        outgoing(8, l, m).start()
+
+    def guarded(fn, l, m, limit):
+        if isinstance(l, int):
+            fn(l, m)
+        else:
+            pl.when(l < limit)(lambda: fn(l, m))
+
+    def load(k, l, m):
+        src = own[m].at[l] if k == 0 else got[m].at[k - 1, l]
+        return pltpu.make_async_copy(src, wb_ref.at[k], load_sem.at[k])
+
+    def normalize(l):
+        def body(i, _):
+            r = pl.ds(pl.multiple_of(i * 64, 64), 64)
+            v = h_ref[r].astype(jnp.float32)
+            v = v * lax.rsqrt(jnp.mean(v * v, axis=-1, keepdims=True) + NORM_EPS)
+            n_ref[r] = (v * gain_ref[pl.ds(l, 1)]).astype(jnp.bfloat16)
+            return 0
+        lax.fori_loop(0, rows // 64, body, 0)
+
+    tile = min(256, width)
+
+    def up_part(k):
+        def body(j, _):
+            cols = pl.ds(pl.multiple_of(j * tile, tile), tile)
+            u = jnp.dot(n_ref[...], wb_ref[k, :, cols], preferred_element_type=jnp.float32)
+            a_ref[k, :, cols] = gelu_tanh(u).astype(jnp.bfloat16)
+            return 0
+        lax.fori_loop(0, width // tile, body, 0)
+
+    def down_part(k):
+        def body(j, _):
+            cols = pl.ds(pl.multiple_of(j * tile, tile), tile)
+            u = jnp.dot(a_ref[k], wb_ref[k, :, cols], preferred_element_type=jnp.float32)
+            if k == 0:
+                acc_ref[:, cols] = u
+            else:
+                acc_ref[:, cols] += u
+            return 0
+        lax.fori_loop(0, d_model // tile, body, 0)
+
+    def residual():
+        def body(i, _):
+            r = pl.ds(pl.multiple_of(i * 64, 64), 64)
+            h_ref[r] = h_ref[r] + acc_ref[r].astype(jnp.bfloat16)
+            return 0
+        lax.fori_loop(0, rows // 64, body, 0)
+
+    def compute(l, m):
+        incoming(7, l, m).wait_recv()
+        load(1, l, m).start()
+        load(2, l, m).start()
+        if m == 0:
+            normalize(l)
+        for k in range(4):
+            if k == 3:
+                incoming(8, l, m).wait_recv()
+                load(3, l, m).start()
+            load(k, l, m).wait()
+            (up_part, down_part)[m](k)
+        if m == 1:
+            residual()
+            feat_ref[l // per_feat] = h_ref[...]
+
+    barrier = pltpu.get_barrier_semaphore()
+    for dev in (x_peer, y_peer, z_peer, mate):
+        pl.semaphore_signal(barrier, inc=1, device_id=dev, device_id_type=MESH)
+    h_ref[...] = x_ref[...]
+    pl.semaphore_wait(barrier, 4)
+
+    for l in range(3):
+        for m in range(2):
+            send_x(l, m)
+            if l == 0:
+                outgoing(7, l, m).start()
+    load(0, 0, 0).start()
+    hop_a(0, 0)
+    hop_b(0, 0)
+    hop_a(0, 1)
+    hop_c(0, 0)
+    hop_b(0, 1)
+    hop_a(1, 0)
+
+    def layer(l, _):
+        for m in range(2):
+            guarded(send_x, l + 3, m, n_layers)
+            guarded(lambda a, b: outgoing(7, a, b).start(), l + 1, m, n_layers)
+            nxt = (l, 1) if m == 0 else (l + 1, 0)
+            guarded(hop_c, nxt[0], nxt[1], n_layers)
+            compute(l, m)
+            guarded(lambda a, b: load(0, a, b).start(), nxt[0], nxt[1], n_layers)
+            guarded(hop_b, l + 1, m, n_layers)
+            nxt = (l + 1, 1) if m == 0 else (l + 2, 0)
+            guarded(hop_a, nxt[0], nxt[1], n_layers)
+        return 0
+
+    lax.fori_loop(0, n_layers, layer, 0)
+
+    def drain(l, _):
+        for m in range(2):
+            for stage in range(9):
+                outgoing(stage, l, m).wait_send()
+        return 0
+
+    lax.fori_loop(0, n_layers, drain, 0)
+
+
+def direct_rows(d_model):
+    return d_model - 8 * seed_rows(d_model)
+
+
+def seed_rows(d_model):
+    return max(16, (d_model // 9) // 16 * 16)
+
+
+def run_teacher(x_teach, w_up_t, w_down_t, gain_t, n_feat):
+    n_layers, d_model, width = w_up_t.shape
+    rows = x_teach.shape[0] * x_teach.shape[1]
+    x_flat = x_teach.reshape(rows, d_model)
+    any_spec = pl.BlockSpec(memory_space=pl.ANY)
+    vmem_spec = pl.BlockSpec(memory_space=pltpu.VMEM)
+    n_ticks = 2 * n_layers
+    feat, _, _ = pl.pallas_call(
+        functools.partial(teacher_kernel, n_layers),
+        name='teacher',
+        out_shape=(jax.ShapeDtypeStruct((n_feat, rows, d_model), jnp.bfloat16),
+                   jax.ShapeDtypeStruct((3, n_layers, d_model, width), jnp.bfloat16),
+                   jax.ShapeDtypeStruct((3, n_layers, width, d_model), jnp.bfloat16)),
+        in_specs=[vmem_spec, vmem_spec, any_spec, any_spec],
+        out_specs=(vmem_spec, any_spec, any_spec),
+        scratch_shapes=[
+            pltpu.VMEM((rows, d_model), jnp.bfloat16),
+            pltpu.VMEM((rows, d_model), jnp.bfloat16),
+            pltpu.VMEM((4, rows, width), jnp.bfloat16),
+            pltpu.VMEM((rows, d_model), jnp.float32),
+            pltpu.VMEM((4, d_model, width), jnp.bfloat16),
+            pltpu.SemaphoreType.DMA((4,)),
+            pltpu.SemaphoreType.DMA((9, n_ticks)),
+            pltpu.SemaphoreType.DMA((9, n_ticks)),
+        ],
+        compiler_params=pltpu.CompilerParams(collective_id=0, has_side_effects=True),
+        cost_estimate=pl.CostEstimate(flops=2 * rows * d_model * width * 4 * 2 * n_layers,
+                                      bytes_accessed=8 * n_layers * d_model * width * 2,
+                                      transcendentals=rows * width * 4 * n_layers),
+    )(x_flat, gain_t, w_up_t, w_down_t)
+    return feat
+
+
 def solution(mesh):
     dp_size = mesh.shape['dp']
     tp_size = mesh.shape['tp']
 
     def local_step(x_teach, x_stud, w_up_t, w_down_t, gain_t, head_t, w_up_s, w_down_s, gain_s, proj_s, head_s):
         n_feat = w_up_s.shape[0]
-        per_feat = w_up_t.shape[0] // n_feat
-        hidden = x_teach
-        features = []
-        for layer_idx in range(w_up_t.shape[0]):
-            normed = (rms_parts(hidden)[0] * gain_t[layer_idx]).astype(jnp.bfloat16)
-            gathered = lax.all_gather(normed, 'tp', axis=1, tiled=True)
-            hidden_act = gelu_tanh(mat_mul('bsd,df->bsf', gathered, w_up_t[layer_idx])).astype(jnp.bfloat16)
-            partial_out = mat_mul('bsf,fd->bsd', hidden_act, w_down_t[layer_idx])
-            layer_out = lax.psum_scatter(partial_out, 'tp', scatter_dimension=1, tiled=True)
-            hidden = hidden + layer_out.astype(jnp.bfloat16)
-            if (layer_idx + 1) % per_feat == 0:
-                features.append(lax.all_to_all(hidden, 'tp', 0, 1, tiled=True))
-        final_norm = rms_parts(hidden)[0].astype(jnp.bfloat16)
-        final_full = lax.all_gather(final_norm, 'tp', axis=1, tiled=True)
+        feats = run_teacher(x_teach, w_up_t, w_down_t, gain_t, n_feat)
+        features = [feats[i].reshape(x_teach.shape) for i in range(n_feat)]
+        x_stud = lax.all_to_all(x_stud, 'tp', 1, 0, tiled=True)
+        final_norm = rms_parts(features[-1])[0].astype(jnp.bfloat16)
+        final_full = lax.all_gather(final_norm, 'tp', axis=0, tiled=True)
         teach_logits = mat_mul('bsd,dv->bsv', final_full, head_t)
 
         n_tokens = x_stud.shape[0] * x_stud.shape[1] * dp_size * tp_size
@@ -118,7 +356,12 @@
         kl_local = jnp.sum(teach_prob * log_ratio)
         logit_grad = (kl_coef * (stud_prob - teach_prob)).astype(jnp.bfloat16)
         head_part = mat_mul('bsd,bsv->dv', stud_full, logit_grad)
-        head_grad = lax.all_gather(lax.psum(head_part, 'dp'), 'tp', axis=1, tiled=True)
+        d_stud = head_s.shape[0]
+        d_pad = -d_stud % (8 * dp_size)
+        head_rows = lax.psum_scatter(jnp.pad(head_part, ((0, d_pad), (0, 0))), 'dp', scatter_dimension=0, tiled=True)
+        head_all = lax.all_gather(head_rows, ('dp', 'tp'), axis=0, tiled=False)
+        head_all = head_all.reshape(dp_size, tp_size, -1, vocab_part).transpose(0, 2, 1, 3)
+        head_grad = head_all.reshape(d_stud + d_pad, tp_size * vocab_part)[:d_stud]
         full_in_grad = mat_mul('bsv,dv->bsd', logit_grad, head_cols)
         head_in_grad = lax.psum_scatter(full_in_grad, 'tp', scatter_dimension=0, tiled=True)
         local_grads = student_backward(saved_acts, w_up_s, w_down_s, gain_s, proj_s, feat_coef, head_in_grad)

time: 2020 us -> 1220 us (0.60)
  waiting for transfers between devices: 1430 us -> 423 us
  Pallas kernels: 0 us -> 329 us
  matrix products: 242 us -> 133 us
  local copies, waits for them, and re-layouts: 104 us -> 141 us
  other arithmetic: 129 us -> 104 us
    reduce_scatter x8 -> x1, waiting for transfers between devices: 558 us -> 144 us  [local_step(): lax.psum_scatter(jnp.pad(head_part, ((0, d_pad), (0, 0))), 'dp', scatter_...]
    pallas_call x0 -> x1, Pallas kernels: none -> 329 us  [run_teacher(): pl.pallas_call(functools.partial(teacher_kernel, n_layers), name='teacher...]
    all_gather x10 -> x2, waiting for transfers between devices: 453 us -> 169 us  [the longest x1 162 us: local_step(): head_all = lax.all_gather(head_rows, ('dp', 'tp'), axis=0, tiled=False)]
    psum x1 -> x0, waiting for transfers between devices: 284 us -> none  [local_step(): lax.psum(head_part, 'dp')]
    dot_general x30 -> x22, matrix products: 242 us -> 133 us  [mat_mul(): jnp.einsum(subscripts, lhs_arr, rhs_arr, preferred_element_type=jnp.float32)]
    reshape x0 -> x1, local copies, waits for them, and re-layouts: none -> 46.3 us  [local_step(): head_grad = head_all.reshape(d_stud + d_pad, tp_size * vocab_part)[:d_stud]]
    transpose x0 -> x1, local copies, waits for them, and re-layouts: none -> 43.9 us  [local_step(): head_all.reshape(dp_size, tp_size, -1, vocab_part).transpose(0, 2, 1, 3)]
    unnamed x82 -> x80, local copies, waits for them, and re-layouts: 59.3 us -> 17.9 us
  transfers between devices with their start and end apart: 23 -> 7, of which waited for: 22 -> 6; matrix products, arithmetic and copies ran while one was open for 8% -> 17% of each run, Pallas kernels for 0% -> 27%
where the time goes in v1:
time: 1220 us; the launch traced here: 1210 us
  waiting for transfers between devices  423 us (35%)
  Pallas kernels  329 us (27%)
  local copies, waits for them, and re-layouts  141 us (12%)
  matrix products  133 us (11%)
  other arithmetic  104 us (9%)
  blocking collectives  61.6 us (5%)
  between operations  17 us (1%)
    pallas_call x1, Pallas kernels, run_teacher(): pl.pallas_call(functools.partial(teacher_kernel, n_layers), name='teacher...  329 us
    all_gather x1, waiting for transfers between devices, local_step(): head_all = lax.all_gather(head_rows, ('dp', 'tp'), axis=0, tiled=False)  162 us
    reduce_scatter x1, waiting for transfers between devices, local_step(): lax.psum_scatter(jnp.pad(head_part, ((0, d_pad), (0, 0))), 'dp', scatter_...  144 us
    dot_general x22, matrix products, mat_mul(): jnp.einsum(subscripts, lhs_arr, rhs_arr, preferred_element_type=jnp.float32)  133 us
    psum x1, waiting for transfers between devices, local_step(): lax.psum(local_grads, ('dp', 'tp'))  74.3 us
    convert_element_type x1, other arithmetic, local_step(): logit_grad = (kl_coef * (stud_prob - teach_prob)).astype(jnp.bfloat16)  51.2 us
    reshape x1, local copies, waits for them, and re-layouts, local_step(): head_grad = head_all.reshape(d_stud + d_pad, tp_size * vocab_part)[:d_stud]  46.3 us
    transpose x1, local copies, waits for them, and re-layouts, local_step(): head_all.reshape(dp_size, tp_size, -1, vocab_part).transpose(0, 2, 1, 3)  43.9 us
  transfers between devices with their start and end apart: 7, of which 6 were waited for; matrix products, arithmetic and copies ran while one was open for 17% of the time, Pallas kernels for 27%

profile of v1, /device:TPU:0, one launch (start us, length us, event | category | flops | bytes accessed | tf_op | source)
XLA Modules:
  0.0 1214.0 jit_solution(4526140516406943127)
XLA Ops:
  9.1 4.3 all-to-all-start
  14.2 6.3 all-to-all-done
  28.9 328.8 %teacher.1 = (bf16[2,512,1024]{2,1,0:T(8,128)(2,1)}, bf16[3,8,1024,1024]{3,2,1,0:T(8,128)(2,1)}, bf16[3,8,1024,1024]{3,2,1,0:T(8,128)(2,1)}) custom-call(bf16[512,1024]{1,0:T(8,128)(2,1)} %bitcast.143, f32[8,1024]{1,0:T(8,128)} %gain_ref.1, bf16[8,1024,1024]{2,1,0:T(8,128)(2,1)} %wu_ref.1, bf16[8,1024,1024]{2,1,0:T(8,128)(2,1)} %wd_ref.1), custom_call_target="tpu_custom_call" | custom-call | flops 68719476736 | bytes 134217728 | tf_op jit(solution)/shard_map/teacher/pallas_call | solution.py:300
  359.2 2.8 slice_convert_fusion
  365.2 28.0 %fusion.64 = (f32[32,64]{1,0:T(8,128)S(1)}, f32[32,64,7648]{2,1,0:T(8,128)}) fusion(bf16[32,64,312]{2,1,0:T(8,128)(2,1)} %all-gather.7.cloned.1.call-done, bf16[312,30592]{1,0:T(8,128)(2,1)} %param.21, s32[]{:T(128)S(6)} %select_n.3), kind=kOutput, calls=%fused_computation.131 | convolution fusion | flops 9789437952 | bytes 69025792 | tf_op jit(solution)/shard_map/bsd,dv->bsv/dot_general | solution.py:32
  393.2 6.8 all-gather.5.cloned.1.call-done
  400.0 41.6 %fusion.65 = (f32[32,64]{1,0:T(8,128)S(1)}, f32[32,64,7648]{2,1,0:T(8,128)}) fusion(bf16[32,64,1024]{2,1,0:T(8,128)(2,1)} %all-gather.5.cloned.1.call-done, bf16[1024,7648]{0,1:T(8,128)(2,1)} %param.16), kind=kOutput, calls=%fused_computation.132 | convolution fusion | flops 32093698048 | bytes 82518016 | tf_op jit(solution)/shard_map/bsd,dv->bsv/dot_general | solution.py:32
  441.7 10.6 pmax.7
  452.3 38.9 %fusion.1 = (f32[32,64]{1,0:T(8,128)S(1)}, f32[32,64]{1,0:T(8,128)S(1)}) fusion(f32[32,64,7648]{2,1,0:T(8,128)} %get-tuple-element.39, f32[32,64]{1,0:T(8,128)S(1)} %get-tuple-element.26, f32[32,64,7648]{2,1,0:T(8,128)} %get-tuple-element.37, f32[32,64]{1,0:T(8,128)S(1)} %get-tuple-element.27), kind=kLoop, calls=%fused_computation.5 | loop fusion | flops 62648320 | bytes 125337600 | tf_op jit(solution)/shard_map/reduce_sum | solution.py:351
  491.3 10.3 psum.42
  501.6 51.2 %multiply_convert_fusion = (bf16[32,64,7648]{2,1,0:T(8,128)(2,1)}, f32[]{:T(128)}) fusion(f32[32,64,7648]{2,1,0:T(8,128)} %get-tuple-element.37, f32[32,64,7648]{2,1,0:T(8,128)} %get-tuple-element.39, f32[32,64]{1,0:T(8,128)S(1)} %get-tuple-element.24, f32[32,64]{1,0:T(8,128)S(1)} %get-tuple-element.25, f32[32,64]{1,0:T(8,128)S(1)} %get-tuple-element.27, ...), kind=kLoop, calls=%fused_computation | loop fusion | flops 172294144 | bytes 156672000 | tf_op jit(solution)/shard_map/convert_element_type | solution.py:357
  552.8 15.8 %convolution_bitcast_fusion = f32[312,7648]{1,0:T(8,128)S(1)} fusion(bf16[32,64,312]{2,1,0:T(8,128)(2,1)} %all-gather.7.cloned.1.call-done, bf16[32,64,7648]{2,1,0:T(8,128)(2,1)} %get-tuple-element.18), kind=kOutput, calls=%fused_computation.9 | convolution fusion | flops 9773776896 | bytes 42148864 | tf_op jit(solution)/shard_map/bsd,bsv->dv/dot_general | solution.py:32
  568.7 5.1 pad.4
  574.1 23.4 %fusion.5 = f32[32,64,312]{2,1,0:T(8,128)} fusion(bf16[32,64,7648]{2,1,0:T(8,128)(2,1)} %get-tuple-element.18, bf16[312,30592]{1,0:T(8,128)(2,1)} %param.21, s32[]{:T(128)S(6)} %select_n.3), kind=kOutput, calls=%fused_computation.10 | convolution fusion | flops 9773776896 | bytes 38805508 | tf_op jit(solution)/shard_map/bsv,dv->bsd/dot_general | solution.py:32
  597.5 144.2 %reduce-scatter.5.cloned.1.call-done = f32[40,7648]{1,0:T(8,128)} async-done(((f32[320,7648]{1,0:T(8,128)}), f32[40,7648]{1,0:T(8,128)}) %reduce-scatter.5.cloned.1.call-update) | async-done | bytes 1223696 | tf_op jit(solution)/shard_map/reduce_scatter | solution.py:361
  752.9 28.6 %reduce-scatter.3.cloned.1.call-done = f32[8,64,312]{2,1,0:T(8,128)} async-done(((f32[32,64,312]{2,1,0:T(8,128)}), f32[8,64,312]{2,1,0:T(8,128)}) %reduce-scatter.3.cloned.1.call-update) | async-done | bytes 638992 | tf_op jit(solution)/shard_map/reduce_scatter | solution.py:366
  784.2 2.5 fusion.24
  803.9 40.7 %all-reduce.1 = (f32[]{:T(128)}, f32[2,312]{1,0:T(2,128)}) all-reduce(f32[]{:T(128)S(6)} %add.111, f32[2,312]{1,0:T(2,128)S(1)} %pad_maximum_fusion.5), channel_id=1, replica_groups=mesh['dp'=8,'tp'=4] {'dp','tp'}, use_global_device_ids=true, to_apply=%region_13.14 | all-reduce | flops 625 | bytes 5000 | tf_op jit(solution)/shard_map/psum | solution.py:369
  844.6 162.2 %all-gather.9.cloned.1.call-done = f32[1280,7648]{1,0:T(8,128)} async-done(((f32[40,7648]{1,0:T(8,128)}), f32[1280,7648]{1,0:T(8,128)}) %all-gather.9.cloned.1.call-update) | async-done | bytes 39157776 | tf_op jit(solution)/shard_map/all_gather | solution.py:362
  1006.8 43.9 %copy.33 = f32[8,40,4,7648]{3,2,1,0:T(4,128)} copy(f32[8,40,4,7648]{3,1,2,0:T(8,128)} %bitcast.131) | data formatting | bytes 78315520 | tf_op jit(solution)/shard_map/transpose | solution.py:363
  1050.7 46.3 %reshape.114 = f32[320,30592]{1,0:T(8,128)} reshape(f32[8,40,4,7648]{3,2,1,0:T(4,128)} %copy.33) | data formatting | bytes 78315520 | tf_op jit(solution)/shard_map/reshape | solution.py:364
  1097.0 27.1 %slice.81 = f32[312,30592]{1,0:T(8,128)} slice(f32[320,30592]{1,0:T(8,128)} %reshape.114), slice={[0:312], [0:30592]} | slice | bytes 76357632 | tf_op jit(solution)/shard_map/slice | solution.py:364
  1124.0 74.3 %all-reduce.5.cloned.1.call-done = (f32[2,312,1248]{2,1,0:T(8,128)}, f32[2,1248,312]{1,2,0:T(8,128)}, f32[2,312,1024]{2,1,0:T(8,128)}) async-done(((f32[2,312,1248]{2,1,0:T(8,128)}, f32[2,1248,312]{1,2,0:T(8,128)}, f32[2,312,1024]{2,1,0:T(8,128)}), (f32[2,312,1248]{2,1,0:T(8,128)}, f32[2,1248,312]{1,2,0:T(8,128)}, f32[2,312,1024]{2,1,0:T(8,128)})) %all-reduce.5.cloned.1.call-update) | async-done | bytes 8785936 | tf_op jit(solution)/shard_map/psum | solution.py:368
  1198.4 3.9 copy.40
  (142 shorter events, 49.1 us)
Async XLA Ops:
  9.1 11.5 all-to-all-start
  13.4 8.2 copy-start.22
  13.4 351.8 %all-gather.7.cloned.1.call-start = ((), (), s32[]{:S(2)}) async-start(), calls=%async_computation.4 | async-start | bytes 1966080 | tf_op jit(solution)/shard_map/all_gather | solution.py:344
  14.2 8.2 copy-start.33
  14.2 9.8 copy-start.31
  24.0 2.6 copy-start.6
  28.8 371.2 %all-gather.5.cloned.1.call-start = ((), (), s32[]{:S(2)}) async-start(), calls=%async_computation.3 | async-start | bytes 5242880 | tf_op jit(solution)/shard_map/all_gather | solution.py:336
  364.6 377.1 %reduce-scatter.5.cloned.1.call-start = ((), (), s32[]{:S(2)}) async-start(), calls=%async_computation.6 | async-start | bytes 11059200 | tf_op jit(solution)/shard_map/reduce_scatter | solution.py:361
  573.8 207.8 %reduce-scatter.3.cloned.1.call-start = ((), (), s32[]{:S(2)}) async-start(), calls=%async_computation.5 | async-start | bytes 3932160 | tf_op jit(solution)/shard_map/reduce_scatter | solution.py:366
  597.5 144.3 %copy-start.30 = (f32[4,2,64]{2,0,1:T(4,128)S(1)}, f32[4,2,64]{2,0,1:T(4,128)}, u32[]{:S(2)}) copy-start(f32[4,2,64]{2,0,1:T(4,128)} %copy-done.29) | copy-start | bytes 6148
  597.5 144.3 %copy-start.1 = (f32[1,512,1024]{2,1,0:T(8,128)S(1)}, f32[1,512,1024]{2,1,0:T(8,128)}, u32[]{:S(2)}) copy-start(f32[1,512,1024]{2,1,0:T(8,128)} %copy-done) | copy-start | bytes 6291460
  597.5 144.4 %copy-start.9 = (bf16[2,312,1024]{2,1,0:T(8,128)(2,1)S(1)}, bf16[2,312,1024]{2,1,0:T(8,128)(2,1)}, u32[]{:S(2)}) copy-start(bf16[2,312,1024]{2,1,0:T(8,128)(2,1)} %param.20) | copy-start | bytes 3833860
  597.5 409.3 %all-gather.9.cloned.1.call-start = ((), (), s32[]{:S(2)}) async-start(), calls=%async_computation.7 | async-start | bytes 40550400 | tf_op jit(solution)/shard_map/all_gather | solution.py:362
  741.7 456.6 %all-reduce.5.cloned.1.call-start = ((), (), s32[]{:S(2)}) async-start(), calls=%async_computation.8 | async-start | bytes 17891328 | tf_op jit(solution)/shard_map/psum | solution.py:368
  744.3 3.7 copy-start.4
  748.7 2.7 copy-start.10
  750.3 31.3 %copy-start.3 = (f32[8,64,312]{2,1,0:T(8,128)S(1)}, f32[8,64,312]{2,1,0:T(8,128)}, u32[]{:S(2)}) copy-start(f32[8,64,312]{2,1,0:T(8,128)} %copy-done.2) | copy-start | bytes 1916932
  750.3 31.3 %copy-start.5 = (f32[8,64,1024]{2,1,0:T(8,128)S(1)}, f32[8,64,1024]{2,1,0:T(8,128)}, u32[]{:S(2)}) copy-start(f32[8,64,1024]{2,1,0:T(8,128)} %copy-done.4) | copy-start | bytes 6291460
  750.3 31.3 %copy-start.26 = (f32[8,64]{1,0:T(8,128)S(1)}, f32[8,64]{1,0:T(8,128)}, u32[]{:S(2)}) copy-start(f32[8,64]{1,0:T(8,128)} %copy-done.25) | copy-start | bytes 6148
  781.6 2.6 copy-start.20
  781.6 2.6 copy-start.36
  784.2 2.6 copy-start.32
  1198.4 3.9 copy-start.13
  1202.3 2.9 copy-start.21
  (21 other events, 36.1 us)
Sparse Core Ops, SparseCore 0:
  28.9 29.1 all-gather.6
  364.7 35.2 all-gather.4
  573.9 167.7 reduce-scatter.4
  744.7 36.8 reduce-scatter.2
  784.3 222.3 all-gather.8
  1013.5 184.8 all-reduce.4

commit v2 on v1

--- a/solution.py
+++ b/solution.py
@@ -323,6 +323,329 @@
     return feat
 
 
+def head_chunk(vocab_part):
+    return 512 if vocab_part > 4096 else 128
+
+
+def stats_kernel(vocab_part, fn_ref, s_ref, wt_ref, ws_ref, st_ref, acct_ref, accs_ref,
+                 mt_ref, zt_ref, ms_ref, zs_ref, w_ref):
+    step = pl.program_id(0)
+    n_steps = pl.num_programs(0)
+    rows, chunk = fn_ref.shape[0], wt_ref.shape[1]
+    blk = min(256, rows)
+
+    @pl.when(step == 0)
+    def _():
+        for ref in (mt_ref, ms_ref):
+            ref[...] = jnp.full_like(ref, -jnp.inf)
+        for ref in (zt_ref, zs_ref, w_ref, acct_ref, accs_ref):
+            ref[...] = jnp.zeros_like(ref)
+
+    def run(masked):
+        ws = ws_ref[...]
+        if masked:
+            valid = step * chunk + lax.broadcasted_iota(jnp.int32, (1, chunk), 1) < vocab_part
+            ws = jnp.where(valid, ws.astype(jnp.float32), 0.0).astype(jnp.bfloat16)
+
+        def fold(logits, r, m_ref, z_ref, acc_ref):
+            m_old = m_ref[r]
+            m_new = jnp.maximum(m_old, jnp.max(logits, axis=1, keepdims=True))
+            scale = jnp.exp(m_old - m_new)
+            e = jnp.exp(logits - m_new)
+            m_ref[r] = m_new
+            z_ref[r] = z_ref[r] * scale + jnp.sum(e, axis=1, keepdims=True)
+            part = lax.dot_general(e.astype(jnp.bfloat16), ws, (((1,), (1,)), ((), ())),
+                                   preferred_element_type=jnp.float32)
+            acc_ref[r] = acc_ref[r] * scale + part
+            return e, scale
+
+        def body(i, _):
+            r = pl.ds(pl.multiple_of(i * blk, blk), blk)
+            lt = jnp.dot(fn_ref[r], wt_ref[...], preferred_element_type=jnp.float32)
+            ls = jnp.dot(s_ref[r], ws, preferred_element_type=jnp.float32)
+            diff = lt - ls
+            if masked:
+                diff = jnp.where(valid, diff, 0.0)
+                lt = jnp.where(valid, lt, -jnp.inf)
+                ls = jnp.where(valid, ls, -jnp.inf)
+            e, scale = fold(lt, r, mt_ref, zt_ref, acct_ref)
+            w_ref[r] = w_ref[r] * scale + jnp.sum(e * diff, axis=1, keepdims=True)
+            fold(ls, r, ms_ref, zs_ref, accs_ref)
+            return 0
+
+        lax.fori_loop(0, rows // blk, body, 0)
+
+    if vocab_part % chunk == 0:
+        run(False)
+    else:
+        pl.when(step < n_steps - 1)(lambda: run(False))
+        pl.when(step == n_steps - 1)(lambda: run(True))
+
+    @pl.when(step == n_steps - 1)
+    def _():
+        lane = lax.broadcasted_iota(jnp.int32, st_ref.shape, 1)
+        out = jnp.zeros(st_ref.shape, jnp.float32)
+        for i, ref in enumerate((mt_ref, zt_ref, ms_ref, zs_ref, w_ref)):
+            out = jnp.where(lane == i, ref[...], out)
+        st_ref[...] = out
+
+
+def head_stats(full_norm, stud_full, head_t, head_cols):
+    rows, d_model = full_norm.shape
+    d_stud = stud_full.shape[1]
+    vocab_part = head_t.shape[1]
+    chunk = head_chunk(vocab_part)
+    n_steps = pl.cdiv(vocab_part, chunk)
+    whole = lambda shape: pl.BlockSpec(shape, lambda i: (0, 0), pipeline_mode=pl.Buffered(1))
+    return pl.pallas_call(
+        functools.partial(stats_kernel, vocab_part),
+        name='head_stats',
+        grid=(n_steps,),
+        out_shape=(jax.ShapeDtypeStruct((rows, 128), jnp.float32),
+                   jax.ShapeDtypeStruct((rows, d_stud), jnp.float32),
+                   jax.ShapeDtypeStruct((rows, d_stud), jnp.float32)),
+        in_specs=[whole((rows, d_model)), whole((rows, d_stud)),
+                  pl.BlockSpec((d_model, chunk), lambda i: (0, i)),
+                  pl.BlockSpec((d_stud, chunk), lambda i: (0, i))],
+        out_specs=(whole((rows, 128)), whole((rows, d_stud)), whole((rows, d_stud))),
+        scratch_shapes=[pltpu.VMEM((rows, 1), jnp.float32)] * 5,
+        cost_estimate=pl.CostEstimate(flops=2 * rows * vocab_part * (d_model + 3 * d_stud),
+                                      bytes_accessed=2 * vocab_part * (d_model + d_stud),
+                                      transcendentals=2 * rows * vocab_part),
+    )(full_norm, stud_full, head_t, head_cols)
+
+
+HEAD_STAGES = 9
+
+
+def head_grad_kernel(vocab_part, n_chunks, kl_coef, fn_ref, s_ref, st_ref, lt_ref, ls_ref, wt_ref, ws_ref, out_ref,
+                     d_ref, part_ref, yb_ref, nb_ref, fb_ref, copy_sem, send_sem, recv_sem):
+    step = pl.program_id(0)
+    rows, chunk = fn_ref.shape[0], wt_ref.shape[1]
+    d_stud = st_ref.shape[0]
+    d_pad = part_ref.shape[1]
+    half, quart, eighth = d_pad // 2, d_pad // 4, d_pad // 8
+    blk = min(256, rows)
+    dp, tp = lax.axis_index('dp'), lax.axis_index('tp')
+    z, y = dp // 2, dp % 2
+    x, c = tp // 2, tp % 2
+    zz, zh = z % 2, z // 2
+    tp_x = (1 - x) * 2 + c
+    x_peer = (dp, tp_x)
+    mate = (dp, x * 2 + 1 - c)
+    y_peer = (z * 2 + 1 - y, tp)
+    near = ((z + 1 - 2 * zz) * 2 + y, tp)
+    far = (((1 - zh) * 2 + zz) * 2 + y, tp)
+
+    def span(yy, n=None, f=None):
+        start, size = yy * half, half
+        if n is not None:
+            start, size = start + n * quart, quart
+        if f is not None:
+            start, size = start + f * eighth, eighth
+        return pl.ds(pl.multiple_of(start, 8), size)
+
+    def cols(i):
+        return pl.ds(pl.multiple_of(i * chunk, chunk), chunk)
+
+    def copy(stage, i, src, dst, dev):
+        return pltpu.make_async_remote_copy(src, dst, send_sem.at[stage, i], recv_sem.at[stage, i],
+                                            device_id=dev, device_id_type=MESH)
+
+    def outgoing(stage, i):
+        g = out_ref.at[tp]
+        if stage == 0:
+            return copy(0, i, part_ref.at[i, span(1 - y)], yb_ref.at[i], y_peer)
+        if stage == 1:
+            return copy(1, i, part_ref.at[i, span(y, 1 - zz)], nb_ref.at[i], near)
+        if stage == 2:
+            return copy(2, i, part_ref.at[i, span(y, zz, 1 - zh)], fb_ref.at[i], far)
+        if stage == 3:
+            r = span(y, zz, zh)
+            return copy(3, i, part_ref.at[i, r], g.at[r, cols(i)], far)
+        if stage == 4:
+            r = span(y, zz)
+            return copy(4, i, g.at[r, cols(i)], g.at[r, cols(i)], near)
+        if stage == 5:
+            r = span(y)
+            return copy(5, i, g.at[r, cols(i)], g.at[r, cols(i)], y_peer)
+        if stage == 6:
+            return copy(6, i, g.at[:, cols(i)], g.at[:, cols(i)], x_peer)
+        if stage == 7:
+            return copy(7, i, g.at[:, cols(i)], g.at[:, cols(i)], mate)
+        gx = out_ref.at[tp_x]
+        return copy(8, i, gx.at[:, cols(i)], gx.at[:, cols(i)], mate)
+
+    def incoming(stage, i):
+        g = out_ref.at[tp]
+        if stage < 3:
+            ref = (yb_ref, nb_ref, fb_ref)[stage].at[i]
+        elif stage < 6:
+            r = (span(y, zz, 1 - zh), span(y, 1 - zz), span(1 - y))[stage - 3]
+            ref = g.at[r, cols(i)]
+        elif stage == 6:
+            ref = out_ref.at[tp_x, :, cols(i)]
+        elif stage == 7:
+            ref = out_ref.at[x * 2 + 1 - c, :, cols(i)]
+        else:
+            ref = out_ref.at[(1 - x) * 2 + 1 - c, :, cols(i)]
+        return copy(stage, i, ref, ref, mate)
+
+    def keep(i):
+        r = span(y, zz, zh)
+        return pltpu.make_async_copy(part_ref.at[i, r], out_ref.at[tp, r, cols(i)], copy_sem.at[i])
+
+    def compute(masked):
+        if masked:
+            valid = step * chunk + lax.broadcasted_iota(jnp.int32, (1, chunk), 1) < vocab_part
+
+        def body(i, _):
+            r = pl.ds(pl.multiple_of(i * blk, blk), blk)
+            lt = jnp.dot(fn_ref[r], wt_ref[...], preferred_element_type=jnp.float32)
+            ls = jnp.dot(s_ref[r], ws_ref[...], preferred_element_type=jnp.float32)
+            shift_t = jnp.concatenate([lt_ref[r]] * (chunk // 128), axis=1)
+            shift_s = jnp.concatenate([ls_ref[r]] * (chunk // 128), axis=1)
+            diff = kl_coef * (jnp.exp(ls - shift_s) - jnp.exp(lt - shift_t))
+            if masked:
+                diff = jnp.where(valid, diff, 0.0)
+            d_ref[r] = diff.astype(jnp.bfloat16)
+            return 0
+
+        lax.fori_loop(0, rows // blk, body, 0)
+        grad = jnp.dot(st_ref[...], d_ref[...], preferred_element_type=jnp.float32)
+        part_ref[step, pl.ds(0, d_stud)] = grad
+        if d_pad > d_stud:
+            part_ref[step, pl.ds(d_stud, d_pad - d_stud)] = jnp.zeros((d_pad - d_stud, chunk), jnp.float32)
+
+    @pl.when(step == 0)
+    def _():
+        barrier = pltpu.get_barrier_semaphore()
+        for dev in (x_peer, y_peer, near, far, mate):
+            pl.semaphore_signal(barrier, inc=1, device_id=dev, device_id_type=MESH)
+        pl.semaphore_wait(barrier, 5)
+
+    if vocab_part % chunk == 0:
+        pl.when(step < n_chunks)(lambda: compute(False))
+    else:
+        pl.when(step < n_chunks - 1)(lambda: compute(False))
+        pl.when(step == n_chunks - 1)(lambda: compute(True))
+
+    def lagged(lag, fn):
+        i = step - lag
+        pl.when((i >= 0) & (i < n_chunks))(lambda: fn(i))
+
+    def add(stage, rng, buf):
+        def fn(i):
+            incoming(stage, i).wait_recv()
+            part_ref[i, rng] += buf[i]
+        return fn
+
+    lagged(1, add(0, span(y), yb_ref))
+    lagged(2, add(1, span(y, zz), nb_ref))
+    lagged(3, add(2, span(y, zz, zh), fb_ref))
+
+    def start_y(i):
+        outgoing(0, i).start()
+
+    def start_near(i):
+        outgoing(1, i).start()
+
+    def start_far(i):
+        outgoing(2, i).start()
+
+    def start_back_far(i):
+        outgoing(3, i).start()
+        keep(i).start()
+
+    def start_back_near(i):
+        incoming(3, i).wait_recv()
+        keep(i).wait()
+        outgoing(4, i).start()
+
+    def start_back_y(i):
+        incoming(4, i).wait_recv()
+        outgoing(5, i).start()
+
+    def start_out(i):
+        incoming(5, i).wait_recv()
+        outgoing(6, i).start()
+        outgoing(7, i).start()
+
+    def start_relay(i):
+        incoming(6, i).wait_recv()
+        outgoing(8, i).start()
+
+    def finish(i):
+        incoming(7, i).wait_recv()
+        incoming(8, i).wait_recv()
+
+    for lag, fn in ((0, start_y), (1, start_near), (2, start_far), (3, start_back_far), (4, start_back_near),
+                    (5, start_back_y), (6, start_out), (7, start_relay), (8, finish)):
+        lagged(lag, fn)
+
+    @pl.when(step == pl.num_programs(0) - 1)
+    def _():
+        def drain(i, _):
+            for stage in range(HEAD_STAGES):
+                outgoing(stage, i).wait_send()
+            return 0
+        lax.fori_loop(0, n_chunks, drain, 0)
+
+
+def head_grads(full_norm, stud_full, log_t, log_s, head_t, head_cols, kl_coef, tp_size):
+    rows, d_model = full_norm.shape
+    d_stud = stud_full.shape[1]
+    vocab_part = head_t.shape[1]
+    chunk = head_chunk(vocab_part)
+    n_chunks = pl.cdiv(vocab_part, chunk)
+    d_pad = pl.cdiv(d_stud, 64) * 64
+    whole = lambda shape: pl.BlockSpec(shape, lambda i: (0, 0), pipeline_mode=pl.Buffered(1))
+    return pl.pallas_call(
+        functools.partial(head_grad_kernel, vocab_part, n_chunks, kl_coef),
+        name='head_grads',
+        grid=(n_chunks + 9,),
+        out_shape=jax.ShapeDtypeStruct((tp_size, d_pad, n_chunks * chunk), jnp.float32),
+        in_specs=[whole((rows, d_model)), whole((rows, d_stud)), whole((d_stud, rows)),
+                  whole((rows, 128)), whole((rows, 128)),
+                  pl.BlockSpec((d_model, chunk), lambda i: (0, jnp.minimum(i, n_chunks - 1))),
+                  pl.BlockSpec((d_stud, chunk), lambda i: (0, jnp.minimum(i, n_chunks - 1)))],
+        out_specs=pl.BlockSpec(memory_space=pl.ANY),
+        scratch_shapes=[
+            pltpu.VMEM((rows, chunk), jnp.bfloat16),
+            pltpu.VMEM((n_chunks, d_pad, chunk), jnp.float32),
+            pltpu.VMEM((n_chunks, d_pad // 2, chunk), jnp.float32),
+            pltpu.VMEM((n_chunks, d_pad // 4, chunk), jnp.float32),
+            pltpu.VMEM((n_chunks, d_pad // 8, chunk), jnp.float32),
+            pltpu.SemaphoreType.DMA((n_chunks,)),
+            pltpu.SemaphoreType.DMA((HEAD_STAGES, n_chunks)),
+            pltpu.SemaphoreType.DMA((HEAD_STAGES, n_chunks)),
+        ],
+        compiler_params=pltpu.CompilerParams(collective_id=1, has_side_effects=True),
+        cost_estimate=pl.CostEstimate(flops=200 * 10**9, bytes_accessed=2 * vocab_part * (d_model + d_stud),
+                                      transcendentals=2 * rows * vocab_part),
+    )(full_norm, stud_full, stud_full.T, jnp.broadcast_to(log_t[:, None], (rows, 128)),
+      jnp.broadcast_to(log_s[:, None], (rows, 128)), head_t, head_cols)
+
+
+def join_kernel(vocab_part, in_ref, out_ref):
+    out_ref[...] = jnp.concatenate([in_ref[q, :, :vocab_part] for q in range(in_ref.shape[0])], axis=1)
+
+
+def join_quarters(parts, d_stud, vocab_part):
+    n_parts, _, padded = parts.shape
+    blk = 24 if d_stud % 24 == 0 else 8
+    return pl.pallas_call(
+        functools.partial(join_kernel, vocab_part),
+        name='join_quarters',
+        grid=(d_stud // blk,),
+        out_shape=jax.ShapeDtypeStruct((d_stud, n_parts * vocab_part), jnp.float32),
+        in_specs=[pl.BlockSpec((n_parts, blk, padded), lambda i: (0, i, 0))],
+        out_specs=pl.BlockSpec((blk, n_parts * vocab_part), lambda i: (i, 0)),
+        cost_estimate=pl.CostEstimate(flops=d_stud * n_parts * vocab_part, transcendentals=0,
+                                      bytes_accessed=8 * d_stud * n_parts * vocab_part),
+    )(parts)
+
+
 def solution(mesh):
     dp_size = mesh.shape['dp']
     tp_size = mesh.shape['tp']
@@ -340,33 +663,37 @@
         feat_coef = 1.0 / (n_feat * n_tokens * head_t.shape[0])
         kl_coef = 1.0 / n_tokens
         saved_acts, err_total = student_forward(x_stud, w_up_s, w_down_s, gain_s, proj_s, features)
+        d_stud, d_teach = x_stud.shape[2], x_teach.shape[2]
+        vocab_part = head_t.shape[1]
+        n_own = x_stud.shape[0] * x_stud.shape[1]
+        tp_idx = lax.axis_index('tp')
         head_in = saved_acts[-1][7]
-        stud_full = lax.all_gather(head_in, 'tp', axis=0, tiled=True)
-        vocab_part = head_t.shape[1]
-        head_cols = lax.dynamic_slice_in_dim(head_s, lax.axis_index('tp') * vocab_part, vocab_part, axis=1)
-        stud_logits = mat_mul('bsd,dv->bsv', stud_full, head_cols)
-        peak_vals = lax.pmax(jnp.stack([jnp.max(teach_logits, axis=-1), jnp.max(stud_logits, axis=-1)]), 'tp')
-        teach_exp = jnp.exp(teach_logits - peak_vals[0][..., None])
-        stud_exp = jnp.exp(stud_logits - peak_vals[1][..., None])
-        sum_vals = lax.psum(jnp.stack([jnp.sum(teach_exp, axis=-1), jnp.sum(stud_exp, axis=-1)]), 'tp')
-        log_norms = peak_vals + jnp.log(sum_vals)
-        teach_prob = teach_exp / sum_vals[0][..., None]
-        stud_prob = stud_exp / sum_vals[1][..., None]
-        log_ratio = teach_logits - stud_logits - (log_norms[0] - log_norms[1])[..., None]
-        kl_local = jnp.sum(teach_prob * log_ratio)
-        logit_grad = (kl_coef * (stud_prob - teach_prob)).astype(jnp.bfloat16)
-        head_part = mat_mul('bsd,bsv->dv', stud_full, logit_grad)
-        d_stud = head_s.shape[0]
-        d_pad = -d_stud % (8 * dp_size)
-        head_rows = lax.psum_scatter(jnp.pad(head_part, ((0, d_pad), (0, 0))), 'dp', scatter_dimension=0, tiled=True)
-        head_all = lax.all_gather(head_rows, ('dp', 'tp'), axis=0, tiled=False)
-        head_all = head_all.reshape(dp_size, tp_size, -1, vocab_part).transpose(0, 2, 1, 3)
-        head_grad = head_all.reshape(d_stud + d_pad, tp_size * vocab_part)[:d_stud]
-        full_in_grad = mat_mul('bsv,dv->bsd', logit_grad, head_cols)
-        head_in_grad = lax.psum_scatter(full_in_grad, 'tp', scatter_dimension=0, tiled=True)
-        local_grads = student_backward(saved_acts, w_up_s, w_down_s, gain_s, proj_s, feat_coef, head_in_grad)
-        grad_up, grad_down, grad_gain, grad_proj = lax.psum(local_grads, ('dp', 'tp'))
-        total_loss = lax.psum(feat_coef * err_total + kl_coef * kl_local, ('dp', 'tp'))
+        stud_full = lax.all_gather(head_in, 'tp', axis=0, tiled=True).reshape(tp_size * n_own, d_stud)
+        full_norm = final_full.reshape(tp_size * n_own, d_teach)
+        head_cols = lax.dynamic_slice_in_dim(head_s, tp_idx * vocab_part, vocab_part, axis=1)
+        stats, acc_t, acc_s = head_stats(full_norm, stud_full, head_t, head_cols)
+        all_stats = lax.all_gather(stats[:, :5].T, 'tp', axis=0)
+        peaks = jnp.max(all_stats[:, 0::2][:, :2], axis=0)
+        scales = jnp.exp(all_stats[:, 0:4:2] - peaks)
+        sums = jnp.sum(all_stats[:, 1:4:2] * scales, axis=0)
+        log_norms = peaks + jnp.log(sums)
+        kl_tokens = (jnp.sum(all_stats[:, 4] * scales[:, 0], axis=0) / sums[0]) - (log_norms[0] - log_norms[1])
+        kl_local = jnp.sum(lax.dynamic_slice_in_dim(kl_tokens, tp_idx * n_own, n_own))
+        own_t = jnp.exp(stats[:, 0] - log_norms[0])[:, None]
+        own_s = jnp.exp(stats[:, 2] - log_norms[1])[:, None]
+        full_in_grad = kl_coef * (acc_s * own_s - acc_t * own_t)
+        head_in_grad = lax.psum_scatter(full_in_grad, 'tp', scatter_dimension=0, tiled=True).reshape(x_stud.shape)
+        grad_up, grad_down, grad_gain, grad_proj = student_backward(
+            saved_acts, w_up_s, w_down_s, gain_s, proj_s, feat_coef, head_in_grad)
+        loss_part = feat_coef * err_total + kl_coef * kl_local
+        extra = jnp.stack([grad_gain, jnp.full_like(grad_gain, loss_part)], axis=-1)
+        packed = jnp.concatenate([grad_proj, extra], axis=-1)
+        log_norms, grad_up, grad_down, packed = lax.optimization_barrier((log_norms, grad_up, grad_down, packed))
+        grad_up, grad_down, packed = lax.psum((grad_up, grad_down, packed), ('dp', 'tp'))
+        parts = head_grads(full_norm, stud_full, log_norms[0], log_norms[1], head_t, head_cols, kl_coef, tp_size)
+        head_grad = join_quarters(parts, d_stud, vocab_part)
+        grad_proj, grad_gain = packed[..., :d_teach], packed[..., d_teach]
+        total_loss = packed[0, 0, d_teach + 1]
         return total_loss, grad_up, grad_down, grad_gain, grad_proj, head_grad
 
     in_specs = (P('dp', 'tp', None), P(('dp', 'tp'), None, None), P(None, None, 'tp'), P(None, 'tp', None),

time: 1220 us -> 1050 us (0.86)
  Pallas kernels: 329 us -> 866 us
  waiting for transfers between devices: 423 us -> 28.7 us
  matrix products: 133 us -> 31.8 us
  local copies, waits for them, and re-layouts: 141 us -> 62.6 us
  other arithmetic: 104 us -> 26.1 us
  blocking collectives: 61.6 us -> 5.78 us
    pallas_call x0 -> x3, Pallas kernels: none -> 533 us  [the longest x1 343 us: head_grads(): pl.pallas_call(functools.partial(head_grad_kernel, vocab_part, n_chunks,...]
    all_gather x2 -> x1, waiting for transfers between devices: 162 us -> 0.01 us  [local_step(): lax.all_gather(head_in, 'tp', axis=0, tiled=True)]
    reduce_scatter x1 -> x0, waiting for transfers between devices: 144 us -> none  [local_step(): lax.psum_scatter(jnp.pad(head_part, ((0, d_pad), (0, 0))), 'dp', scatter_...]
    dot_general x22 -> x18, matrix products: 133 us -> 31.8 us  [mat_mul(): jnp.einsum(subscripts, lhs_arr, rhs_arr, preferred_element_type=jnp.float32)]
    psum x1, waiting for transfers between devices: 74.3 us -> 0.01 us  [local_step(): lax.psum((grad_up, grad_down, packed), ('dp', 'tp'))]
    convert_element_type x2 -> x0, other arithmetic: 54.1 us -> none  [the longest x1 51.2 us: local_step(): logit_grad = (kl_coef * (stud_prob - teach_prob)).astype(jnp.bfloat16)]
    psum x2 -> x0, blocking collectives: 51 us -> none  [the longest x1 40.7 us: local_step(): lax.psum(feat_coef * err_total + kl_coef * kl_local, ('dp', 'tp'))]
    transpose x1 -> x0, local copies, waits for them, and re-layouts: 43.9 us -> none  [local_step(): head_all.reshape(dp_size, tp_size, -1, vocab_part).transpose(0, 2, 1, 3)]
  transfers between devices with their start and end apart: 7 -> 5, of which waited for: 6 -> 3; matrix products, arithmetic and copies ran while one was open for 17% -> 5% of each run, Pallas kernels for 27% -> 68%
where the time goes in v2:
time: 1050 us; the launch traced here: 1040 us
  Pallas kernels  866 us (82%)
  local copies, waits for them, and re-layouts  62.6 us (6%)
  matrix products  31.8 us (3%)
  waiting for transfers between devices  28.7 us (3%)
  other arithmetic  26.1 us (2%)
  between operations  16.8 us (2%)
    pallas_call x1, Pallas kernels, head_grads(): pl.pallas_call(functools.partial(head_grad_kernel, vocab_part, n_chunks,...  343 us
    pallas_call x1, Pallas kernels, run_teacher(): pl.pallas_call(functools.partial(teacher_kernel, n_layers), name='teacher...  333 us
    pallas_call x1, Pallas kernels, head_stats(): pl.pallas_call(functools.partial(stats_kernel, vocab_part), name='head_st...  158 us
    unnamed x88, local copies, waits for them, and re-layouts  37.3 us
    pallas_call x1, Pallas kernels, join_quarters(): pl.pallas_call(functools.partial(join_kernel, vocab_part), name='join_qua...  32 us
    dot_general x18, matrix products, mat_mul(): jnp.einsum(subscripts, lhs_arr, rhs_arr, preferred_element_type=jnp.float32)  31.8 us
  transfers between devices with their start and end apart: 5, of which 3 were waited for; matrix products, arithmetic and copies ran while one was open for 5% of the time, Pallas kernels for 68%

profile of v2, /device:TPU:0, one launch (start us, length us, event | category | flops | bytes accessed | tf_op | source)
XLA Modules:
  0.0 1042.7 jit_solution(10093971088483009792)
XLA Ops:
  9.1 4.2 all-to-all-start
  14.2 6.5 all-to-all-done
  29.0 333.1 %teacher.1 = (bf16[2,512,1024]{2,1,0:T(8,128)(2,1)}, bf16[3,8,1024,1024]{3,2,1,0:T(8,128)(2,1)}, bf16[3,8,1024,1024]{3,2,1,0:T(8,128)(2,1)}) custom-call(bf16[512,1024]{1,0:T(8,128)(2,1)} %bitcast.132, f32[8,1024]{1,0:T(8,128)} %gain_ref.1, bf16[8,1024,1024]{2,1,0:T(8,128)(2,1)} %wu_ref.1, bf16[8,1024,1024]{2,1,0:T(8,128)(2,1)} %wd_ref.1), custom_call_target="tpu_custom_call" | custom-call | flops 68719476736 | bytes 134217728 | tf_op jit(solution)/shard_map/teacher/pallas_call | solution.py:300
  363.7 2.8 fusion.55
  368.2 20.7 %copy.46.wt_ref = bf16[1024,7648]{1,0:T(8,128)(2,1)} copy(bf16[1024,7648]{0,1:T(8,128)(2,1)} %param.16) | data formatting | bytes 31326208 | tf_op args[5]
  388.9 6.3 constant_dynamic-slice_fusion.ws_ref
  395.2 7.8 all-gather.5.cloned.1.call-done
  403.0 158.0 %head_stats.1 = (f32[2048,128]{1,0:T(8,128)}, f32[2048,312]{1,0:T(8,128)}, f32[2048,312]{1,0:T(8,128)}) custom-call(bf16[2048,1024]{1,0:T(8,128)(2,1)} %bitcast.130, bf16[2048,312]{1,0:T(8,128)(2,1)} %bitcast.124, bf16[1024,7648]{1,0:T(8,128)(2,1)} %copy.46.wt_ref, bf16[312,7648]{1,0:T(8,128)(2,1)} %constant_dynamic-slice_fusion.ws_ref), custom_call_target="tpu_custom_call" | custom-call | flops 61399367680 | bytes 20435456 | tf_op jit(solution)/shard_map/head_stats/pallas_call | solution.py:400
  562.6 5.8 all-gather.1
  574.1 2.9 fusion.18
  579.8 4.5 multiply_reduce_fusion.1
  584.3 2.6 multiply_reduce_fusion
  588.6 2.3 convolution_bitcast_fusion.4
  596.5 3.1 copy.55
  602.9 14.3 %reduce-scatter.2.cloned.1.call-done = f32[512,312]{1,0:T(8,128)} async-done(((f32[2048,312]{1,0:T(8,128)}), f32[512,312]{1,0:T(8,128)}) %reduce-scatter.2.cloned.1.call-update) | async-done | bytes 638992 | tf_op jit(solution)/shard_map/reduce_scatter | solution.py:685
  617.2 2.9 multiply_reduce_fusion.6
  620.5 2.3 fusion.13
  628.6 2.2 fusion.6
  630.8 2.3 convolution_bitcast_fusion.1
  636.1 3.9 pad_maximum_fusion
  641.9 4.1 concatenate.3
  649.6 343.0 %head_grads.1.in_ref = f32[4,320,7680]{2,1,0:T(8,128)} custom-call(bf16[2048,1024]{1,0:T(8,128)(2,1)} %bitcast.131, bf16[2048,312]{1,0:T(8,128)(2,1)} %bitcast.126, bf16[312,2048]{1,0:T(8,128)(2,1)} %bitcast.127, f32[2048,128]{1,0:T(8,128)} %broadcast_in_dim.9.lt_ref, f32[2048,128]{1,0:T(8,128)} %broadcast_in_dim.11.ls_ref, bf16[1024,7648]{1,0:T(8,128)(2,1)} %copy.46.wt_ref, ...), custom_call_target="tpu_custom_call" | custom-call | flops 199999995904 | bytes 20435456 | tf_op jit(solution)/shard_map/head_grads/pallas_call | solution.py:603
  992.6 32.0 %join_quarters.1 = f32[312,30592]{1,0:T(8,128)} custom-call(f32[4,320,7680]{2,1,0:T(8,128)} %head_grads.1.in_ref), custom_call_target="tpu_custom_call" | custom-call | flops 9544704 | bytes 76357632 | tf_op jit(solution)/shard_map/join_quarters/pallas_call | solution.py:637
  1027.6 3.7 slice.125
  (150 shorter events, 54.6 us)
Async XLA Ops:
  9.1 11.6 %all-to-all-start = ((bf16[2,256,312]{2,0,1:T(2,128)(2,1)}), bf16[2,256,312]{2,0,1:T(2,128)(2,1)S(1)}, u32[]{:S(2)}, u32[]{:S(2)}) async-start(bf16[2,256,312]{2,0,1:T(2,128)(2,1)} %copy.42), calls=%async_computation | async-start | bytes 786432 | tf_op jit(solution)/shard_map/all_to_all | solution.py:657
  13.3 8.4 copy-start.23
  13.3 381.9 %all-gather.7.cloned.1.call-start = ((), (), s32[]{:S(2)}) async-start(), calls=%async_computation.3 | async-start | bytes 1966080 | tf_op jit(solution)/shard_map/all_gather | solution.py:671
  14.2 8.4 copy-start.36
  14.2 9.9 copy-start.34
  29.0 374.0 %all-gather.5.cloned.1.call-start = ((), (), s32[]{:S(2)}) async-start(), calls=%async_computation.2 | async-start | bytes 5242880 | tf_op jit(solution)/shard_map/all_gather | solution.py:659
  367.7 249.5 %reduce-scatter.2.cloned.1.call-start = ((), (), s32[]{:S(2)}) async-start(), calls=%async_computation.4 | async-start | bytes 3932160 | tf_op jit(solution)/shard_map/reduce_scatter | solution.py:685
  572.3 4.8 copy-start.17
  574.1 2.9 copy-start.16
  579.1 5.2 copy-start.10
  579.2 445.4 %all-reduce.3.cloned.1.call-start = ((), (), s32[]{:S(2)}) async-start(), calls=%async_computation.5 | async-start | bytes 18530304 | tf_op jit(solution)/shard_map/psum | solution.py:692
  579.8 4.5 copy-start.8
  586.9 3.9 copy-start.3
  591.5 2.8 copy-start.4
  591.5 3.4 copy-start.9
  594.9 4.7 copy-start.27
  594.9 5.7 copy-start.2
  596.5 20.7 %copy-start.1 = (f32[8,64,312]{2,1,0:T(8,128)S(1)}, f32[8,64,312]{2,1,0:T(8,128)}, u32[]{:S(2)}) copy-start(f32[8,64,312]{2,1,0:T(8,128)} %copy-done) | copy-start | bytes 1916932
  596.5 20.7 %copy-start.29 = (f32[8,64]{1,0:T(8,128)S(1)}, f32[8,64]{1,0:T(8,128)}, u32[]{:S(2)}) copy-start(f32[8,64]{1,0:T(8,128)} %copy-done.28) | copy-start | bytes 6148
  617.2 3.2 copy-start.21
  617.2 3.3 copy-start.39
  636.1 3.9 copy-start.22
  1027.6 3.7 copy-start.12
  1031.2 3.1 copy-start.11
  (21 other events, 32.5 us)
Sparse Core Ops, SparseCore 0:
  29.1 29.1 all-gather.6
  367.8 35.1 all-gather.4
  579.3 37.8 reduce-scatter.1
  647.1 280.1 all-reduce.2

commit v3 on v2

--- a/solution.py
+++ b/solution.py
@@ -32,11 +32,10 @@
     return jnp.einsum(subscripts, lhs_arr, rhs_arr, preferred_element_type=jnp.float32)
 
 
-def student_forward(x_stud, w_up_s, w_down_s, gain_s, proj_s, features):
+def student_forward(x_stud, w_up_s, w_down_s, gain_s):
     residual = x_stud.astype(jnp.float32)
     norm_cur, inv_cur = rms_parts(residual)
     saved_acts = []
-    err_total = jnp.zeros((), jnp.float32)
     for layer_idx in range(w_up_s.shape[0]):
         normed = (norm_cur * gain_s[layer_idx]).astype(jnp.bfloat16)
         pre_act = mat_mul('bsd,df->bsf', normed, w_up_s[layer_idx])
@@ -44,25 +43,34 @@
         residual = residual + mat_mul('bsf,fd->bsd', hidden_act, w_down_s[layer_idx])
         norm_next, inv_next = rms_parts(residual)
         proj_in = norm_next.astype(jnp.bfloat16)
+        saved_acts.append((norm_cur, inv_cur, normed, pre_act, hidden_act, norm_next, inv_next, proj_in))
+        norm_cur, inv_cur = norm_next, inv_next
+    return saved_acts
+
+
+def student_errors(saved_acts, proj_s, features, feat_coef):
+    err_total = jnp.zeros((), jnp.float32)
+    err_grads = []
+    proj_grads = []
+    for layer_idx, acts in enumerate(saved_acts):
+        proj_in = acts[7]
         feat_err = mat_mul('bsd,de->bse', proj_in, proj_s[layer_idx]) - features[layer_idx]
         err_total = err_total + jnp.sum(feat_err * feat_err)
-        saved_acts.append((norm_cur, inv_cur, normed, pre_act, hidden_act, norm_next, inv_next, proj_in, feat_err))
-        norm_cur, inv_cur = norm_next, inv_next
-    return saved_acts, err_total
-
-
-def student_backward(saved_acts, w_up_s, w_down_s, gain_s, proj_s, feat_coef, head_in_grad):
+        err_grad = (2.0 * feat_coef * feat_err).astype(jnp.bfloat16)
+        proj_grads.append(mat_mul('bsd,bse->de', proj_in, err_grad))
+        err_grads.append(err_grad)
+    return err_grads, err_total, jnp.stack(proj_grads)
+
+
+def student_backward(saved_acts, w_up_s, w_down_s, gain_s, proj_s, err_grads, head_in_grad):
     n_layers = len(saved_acts)
     up_grads = []
     down_grads = []
     gain_grads = []
-    proj_grads = []
     resid_grad = None
     for layer_idx in reversed(range(n_layers)):
-        norm_cur, inv_cur, normed, pre_act, hidden_act, norm_next, inv_next, proj_in, feat_err = saved_acts[layer_idx]
-        err_grad = (2.0 * feat_coef * feat_err).astype(jnp.bfloat16)
-        proj_grads.append(mat_mul('bsd,bse->de', proj_in, err_grad))
-        out_grad = mat_mul('bse,de->bsd', err_grad, proj_s[layer_idx])
+        norm_cur, inv_cur, normed, pre_act, hidden_act, norm_next, inv_next, proj_in = saved_acts[layer_idx]
+        out_grad = mat_mul('bse,de->bsd', err_grads[layer_idx], proj_s[layer_idx])
         if resid_grad is None:
             resid_grad = rms_back(norm_next, inv_next, out_grad + head_in_grad)
         else:
@@ -76,8 +84,7 @@
         gain_grads.append(jnp.sum(norm_grad * norm_cur, axis=(0, 1)))
         if layer_idx > 0:
             resid_grad = resid_grad + rms_back(norm_cur, inv_cur, norm_grad * gain_s[layer_idx])
-    return (jnp.stack(up_grads[::-1]), jnp.stack(down_grads[::-1]),
-            jnp.stack(gain_grads[::-1]), jnp.stack(proj_grads[::-1]))
+    return jnp.stack(up_grads[::-1]), jnp.stack(down_grads[::-1]), jnp.stack(gain_grads[::-1])
 
 
 MESH = pl.DeviceIdType.MESH
@@ -85,8 +92,12 @@
 N_SEED = 112
 
 
-def teacher_kernel(n_layers, x_ref, gain_ref, wu_ref, wd_ref, feat_ref, gu_ref, gd_ref,
-                   h_ref, n_ref, a_ref, acc_ref, wb_ref, load_sem, send_sem, recv_sem):
+def stud_chunk(vocab):
+    return 2048 if vocab > 16384 else 256
+
+
+def teacher_kernel(n_layers, x_ref, gain_ref, s_ref, wu_ref, wd_ref, hs_ref, feat_ref, lse_ref, ds_ref, gu_ref, gd_ref,
+                   h_ref, n_ref, a_ref, acc_ref, wb_ref, hb_ref, m_ref, z_ref, load_sem, hs_sem, send_sem, recv_sem):
     rows, d_model = x_ref.shape
     width = wu_ref.shape[2]
     per_feat = n_layers // feat_ref.shape[0]
@@ -239,6 +250,56 @@
             residual()
             feat_ref[l // per_feat] = h_ref[...]
 
+    vocab = hs_ref.shape[1]
+    v_chunk = hb_ref.shape[2]
+    n_v = pl.cdiv(vocab, v_chunk)
+    v_tail = vocab - (n_v - 1) * v_chunk
+
+    def load_head(t, slot, act):
+        def go(width):
+            cols = pl.ds(pl.multiple_of(t * v_chunk, 128), width)
+            act(pltpu.make_async_copy(hs_ref.at[:, cols], hb_ref.at[slot, :, pl.ds(0, width)], hs_sem.at[slot]))
+        if v_tail == v_chunk:
+            pl.when(t < n_v)(lambda: go(v_chunk))
+        else:
+            pl.when(t < n_v - 1)(lambda: go(v_chunk))
+            pl.when(t == n_v - 1)(lambda: go(v_tail))
+
+    v_blk = min(512, v_chunk)
+
+    def student_part(t, slot):
+        load_head(t, slot, lambda cp: cp.wait())
+
+        def body(j, _):
+            cols = pl.ds(pl.multiple_of(j * v_blk, v_blk), v_blk)
+            hs = hb_ref[slot, :, cols]
+            limit = vocab - t * v_chunk - j * v_blk
+            valid = lax.broadcasted_iota(jnp.int32, (1, v_blk), 1) < limit
+            logits = jnp.dot(s_ref[...], hs, preferred_element_type=jnp.float32)
+            logits = jnp.where(valid, logits, -jnp.inf)
+            m_old = m_ref[...]
+            m_new = jnp.maximum(m_old, jnp.max(logits, axis=1, keepdims=True))
+            scale = jnp.exp(m_old - m_new)
+            e = jnp.exp(logits - m_new)
+            m_ref[...] = m_new
+            z_ref[...] = z_ref[...] * scale + jnp.sum(e, axis=1, keepdims=True)
+            part = lax.dot_general(e.astype(jnp.bfloat16), hs, (((1,), (1,)), ((), ())),
+                                   preferred_element_type=jnp.float32)
+            ds_ref[...] = ds_ref[...] * scale + part
+            return 0
+
+        n_blk = (jnp.minimum(v_chunk, vocab - t * v_chunk) + v_blk - 1) // v_blk
+
+        @pl.when(t < n_v)
+        def _():
+            lax.fori_loop(0, n_blk, body, 0)
+
+    m_ref[...] = jnp.full_like(m_ref, -jnp.inf)
+    z_ref[...] = jnp.zeros_like(z_ref)
+    ds_ref[...] = jnp.zeros_like(ds_ref)
+    hb_ref[...] = jnp.zeros_like(hb_ref)
+    load_head(0, 0, lambda cp: cp.start())
+
     barrier = pltpu.get_barrier_semaphore()
     for dev in (x_peer, y_peer, z_peer, mate):
         pl.semaphore_signal(barrier, inc=1, device_id=dev, device_id_type=MESH)
@@ -267,11 +328,16 @@
             compute(l, m)
             guarded(lambda a, b: load(0, a, b).start(), nxt[0], nxt[1], n_layers)
             guarded(hop_b, l + 1, m, n_layers)
+            t = 2 * l + m
+            load_head(t + 1, 1 - m, lambda cp: cp.start())
+            student_part(t, m)
             nxt = (l + 1, 1) if m == 0 else (l + 2, 0)
             guarded(hop_a, nxt[0], nxt[1], n_layers)
         return 0
 
     lax.fori_loop(0, n_layers, layer, 0)
+    lse_ref[...] = m_ref[...] + jnp.log(z_ref[...])
+    ds_ref[...] = ds_ref[...] / z_ref[...]
 
     def drain(l, _):
         for m in range(2):
@@ -290,28 +356,36 @@
     return max(16, (d_model // 9) // 16 * 16)
 
 
-def run_teacher(x_teach, w_up_t, w_down_t, gain_t, n_feat):
+def run_teacher(x_teach, w_up_t, w_down_t, gain_t, n_feat, s_own, head_s):
     n_layers, d_model, width = w_up_t.shape
     rows = x_teach.shape[0] * x_teach.shape[1]
     x_flat = x_teach.reshape(rows, d_model)
     any_spec = pl.BlockSpec(memory_space=pl.ANY)
     vmem_spec = pl.BlockSpec(memory_space=pltpu.VMEM)
     n_ticks = 2 * n_layers
-    feat, _, _ = pl.pallas_call(
+    d_stud, vocab = head_s.shape
+    v_chunk = stud_chunk(vocab)
+    feat, lse_s, in_grad_s, _, _ = pl.pallas_call(
         functools.partial(teacher_kernel, n_layers),
         name='teacher',
         out_shape=(jax.ShapeDtypeStruct((n_feat, rows, d_model), jnp.bfloat16),
+                   jax.ShapeDtypeStruct((rows, 1), jnp.float32),
+                   jax.ShapeDtypeStruct((rows, d_stud), jnp.float32),
                    jax.ShapeDtypeStruct((3, n_layers, d_model, width), jnp.bfloat16),
                    jax.ShapeDtypeStruct((3, n_layers, width, d_model), jnp.bfloat16)),
-        in_specs=[vmem_spec, vmem_spec, any_spec, any_spec],
-        out_specs=(vmem_spec, any_spec, any_spec),
+        in_specs=[vmem_spec, vmem_spec, vmem_spec, any_spec, any_spec, any_spec],
+        out_specs=(vmem_spec, vmem_spec, vmem_spec, any_spec, any_spec),
         scratch_shapes=[
             pltpu.VMEM((rows, d_model), jnp.bfloat16),
             pltpu.VMEM((rows, d_model), jnp.bfloat16),
             pltpu.VMEM((4, rows, width), jnp.bfloat16),
             pltpu.VMEM((rows, d_model), jnp.float32),
             pltpu.VMEM((4, d_model, width), jnp.bfloat16),
+            pltpu.VMEM((2, d_stud, v_chunk), jnp.bfloat16),
+            pltpu.VMEM((rows, 1), jnp.float32),
+            pltpu.VMEM((rows, 1), jnp.float32),
             pltpu.SemaphoreType.DMA((4,)),
+            pltpu.SemaphoreType.DMA((2,)),
             pltpu.SemaphoreType.DMA((9, n_ticks)),
             pltpu.SemaphoreType.DMA((9, n_ticks)),
         ],
@@ -319,109 +393,213 @@
         cost_estimate=pl.CostEstimate(flops=2 * rows * d_model * width * 4 * 2 * n_layers,
                                       bytes_accessed=8 * n_layers * d_model * width * 2,
                                       transcendentals=rows * width * 4 * n_layers),
-    )(x_flat, gain_t, w_up_t, w_down_t)
-    return feat
+    )(x_flat, gain_t, s_own, w_up_t, w_down_t, head_s)
+    return feat, lse_s, in_grad_s
 
 
 def head_chunk(vocab_part):
     return 512 if vocab_part > 4096 else 128
 
 
-def stats_kernel(vocab_part, fn_ref, s_ref, wt_ref, ws_ref, st_ref, acct_ref, accs_ref,
-                 mt_ref, zt_ref, ms_ref, zs_ref, w_ref):
-    step = pl.program_id(0)
-    n_steps = pl.num_programs(0)
-    rows, chunk = fn_ref.shape[0], wt_ref.shape[1]
-    blk = min(256, rows)
-
-    @pl.when(step == 0)
-    def _():
-        for ref in (mt_ref, ms_ref):
-            ref[...] = jnp.full_like(ref, -jnp.inf)
-        for ref in (zt_ref, zs_ref, w_ref, acct_ref, accs_ref):
-            ref[...] = jnp.zeros_like(ref)
-
-    def run(masked):
-        ws = ws_ref[...]
-        if masked:
-            valid = step * chunk + lax.broadcasted_iota(jnp.int32, (1, chunk), 1) < vocab_part
-            ws = jnp.where(valid, ws.astype(jnp.float32), 0.0).astype(jnp.bfloat16)
-
-        def fold(logits, r, m_ref, z_ref, acc_ref):
-            m_old = m_ref[r]
-            m_new = jnp.maximum(m_old, jnp.max(logits, axis=1, keepdims=True))
+def grad_chunk(vocab_part):
+    return 256 if vocab_part > 4096 else 128
+
+
+def stats_kernel(vocab_part, h_ref, wt_hbm, ws_ref, fn_hbm, lse_ref, dt_ref,
+                 fn_ref, wt_ref, la_ref, lb_ref, e_ref, sc_ref, m_ref, z_ref, acc_ref, got_ref,
+                 load_sem, out_sem, send_sem, recv_sem):
+    rows, d_model = h_ref.shape
+    d_stud, padded = ws_ref.shape
+    chunk = la_ref.shape[1]
+    n_chunks = padded // chunk
+    width = acc_ref.shape[2]
+    dp, tp = lax.axis_index('dp'), lax.axis_index('tp')
+    x, c = tp // 2, tp % 2
+    tp_m, tp_x, tp_xm = x * 2 + 1 - c, (1 - x) * 2 + c, (1 - x) * 2 + 1 - c
+    peers = ((dp, tp_m), (dp, tp_x), (dp, tp_xm))
+    tail = vocab_part - (n_chunks - 1) * chunk
+
+    def copy(stage, src, dst, dev):
+        return pltpu.make_async_remote_copy(src, dst, send_sem.at[stage], recv_sem.at[stage],
+                                            device_id=dev, device_id_type=MESH)
+
+    to_mate = copy(0, fn_ref.at[tp], fn_ref.at[tp], peers[0])
+    to_x = copy(1, fn_ref.at[tp], fn_ref.at[tp], peers[1])
+    relay = copy(2, fn_ref.at[tp_x], fn_ref.at[tp_x], peers[0])
+    from_mate = copy(0, fn_ref.at[tp_m], fn_ref.at[tp_m], peers[0])
+    from_x = copy(1, fn_ref.at[tp_x], fn_ref.at[tp_x], peers[1])
+    from_relay = copy(2, fn_ref.at[tp_xm], fn_ref.at[tp_xm], peers[0])
+    back = [copy(3 + i, acc_ref.at[1 + i], got_ref.at[i], peers[i]) for i in range(3)]
+
+    def load(j, size):
+        r = pl.ds(pl.multiple_of(j * chunk, 16), size)
+        return pltpu.make_async_copy(wt_hbm.at[r], wt_ref.at[r], load_sem.at[j])
+
+    def load_wait(j):
+        if tail == chunk:
+            load(j, chunk).wait()
+        else:
+            pl.when(j < n_chunks - 1)(lambda: load(j, chunk).wait())
+            pl.when(j == n_chunks - 1)(lambda: load(j, tail).wait())
+
+    barrier = pltpu.get_barrier_semaphore()
+    for dev in peers:
+        pl.semaphore_signal(barrier, inc=1, device_id=dev, device_id_type=MESH)
+
+    def load_start(j, _):
+        load(j, chunk).start()
+        return 0
+
+    lax.fori_loop(0, n_chunks - 1, load_start, 0)
+    load(n_chunks - 1, tail).start()
+    if tail < chunk:
+        wt_ref[pl.ds(vocab_part, chunk - tail)] = jnp.zeros((chunk - tail, d_model), jnp.bfloat16)
+
+    def normalize(i, _):
+        r = pl.ds(pl.multiple_of(i * 64, 64), 64)
+        v = h_ref[r].astype(jnp.float32)
+        v = v * lax.rsqrt(jnp.mean(v * v, axis=-1, keepdims=True) + NORM_EPS)
+        fn_ref[tp, r] = v.astype(jnp.bfloat16)
+        return 0
+
+    lax.fori_loop(0, rows // 64, normalize, 0)
+    m_ref[...] = jnp.full_like(m_ref, -jnp.inf)
+    z_ref[...] = jnp.zeros_like(z_ref)
+    acc_ref[...] = jnp.zeros_like(acc_ref)
+    pl.semaphore_wait(barrier, 3)
+    to_x.start()
+    to_mate.start()
+
+    def logits(q, j, buf, first):
+        if first:
+            load_wait(j)
+        w = wt_ref[pl.ds(pl.multiple_of(j * chunk, chunk), chunk)]
+        buf[...] = lax.dot_general(fn_ref[q], w, (((1,), (1,)), ((), ())), preferred_element_type=jnp.float32)
+
+    def fold(g, j, buf):
+        ws = ws_ref[:, pl.ds(pl.multiple_of(j * chunk, chunk), chunk)]
+        valid = lax.broadcasted_iota(jnp.int32, (1, chunk), 1) < vocab_part - j * chunk
+        for i in range(rows // 64):
+            r = pl.ds(i * 64, 64)
+            v = jnp.where(valid, buf[r], -jnp.inf)
+            m_old = m_ref[g, r]
+            m_new = jnp.maximum(m_old, jnp.max(v, axis=1, keepdims=True))
             scale = jnp.exp(m_old - m_new)
-            e = jnp.exp(logits - m_new)
-            m_ref[r] = m_new
-            z_ref[r] = z_ref[r] * scale + jnp.sum(e, axis=1, keepdims=True)
-            part = lax.dot_general(e.astype(jnp.bfloat16), ws, (((1,), (1,)), ((), ())),
-                                   preferred_element_type=jnp.float32)
-            acc_ref[r] = acc_ref[r] * scale + part
-            return e, scale
-
-        def body(i, _):
-            r = pl.ds(pl.multiple_of(i * blk, blk), blk)
-            lt = jnp.dot(fn_ref[r], wt_ref[...], preferred_element_type=jnp.float32)
-            ls = jnp.dot(s_ref[r], ws, preferred_element_type=jnp.float32)
-            diff = lt - ls
-            if masked:
-                diff = jnp.where(valid, diff, 0.0)
-                lt = jnp.where(valid, lt, -jnp.inf)
-                ls = jnp.where(valid, ls, -jnp.inf)
-            e, scale = fold(lt, r, mt_ref, zt_ref, acct_ref)
-            w_ref[r] = w_ref[r] * scale + jnp.sum(e * diff, axis=1, keepdims=True)
-            fold(ls, r, ms_ref, zs_ref, accs_ref)
+            e = jnp.exp(v - m_new)
+            m_ref[g, r] = m_new
+            z_ref[g, r] = z_ref[g, r] * scale + jnp.sum(e, axis=1, keepdims=True)
+            sc_ref[r] = scale
+            e_ref[r] = e.astype(jnp.bfloat16)
+        part = lax.dot_general(e_ref[...], ws, (((1,), (1,)), ((), ())), preferred_element_type=jnp.float32)
+        acc_ref[g, :, pl.ds(0, d_stud)] = acc_ref[g, :, pl.ds(0, d_stud)] * sc_ref[...] + part
+
+    def group(g, q, first=False):
+        logits(q, 0, la_ref, first)
+
+        def pair(i, _):
+            logits(q, 2 * i + 1, lb_ref, first)
+            fold(g, 2 * i, la_ref)
+            logits(q, 2 * i + 2, la_ref, first)
+            fold(g, 2 * i + 1, lb_ref)
             return 0
 
-        lax.fori_loop(0, rows // blk, body, 0)
-
-    if vocab_part % chunk == 0:
-        run(False)
-    else:
-        pl.when(step < n_steps - 1)(lambda: run(False))
-        pl.when(step == n_steps - 1)(lambda: run(True))
-
-    @pl.when(step == n_steps - 1)
-    def _():
-        lane = lax.broadcasted_iota(jnp.int32, st_ref.shape, 1)
-        out = jnp.zeros(st_ref.shape, jnp.float32)
-        for i, ref in enumerate((mt_ref, zt_ref, ms_ref, zs_ref, w_ref)):
-            out = jnp.where(lane == i, ref[...], out)
-        st_ref[...] = out
-
-
-def head_stats(full_norm, stud_full, head_t, head_cols):
-    rows, d_model = full_norm.shape
-    d_stud = stud_full.shape[1]
-    vocab_part = head_t.shape[1]
+        n_pairs = (n_chunks - 1) // 2
+        lax.fori_loop(0, n_pairs, pair, 0)
+        if n_chunks % 2:
+            fold(g, n_chunks - 1, la_ref)
+        else:
+            logits(q, n_chunks - 1, lb_ref, first)
+            fold(g, n_chunks - 2, la_ref)
+            fold(g, n_chunks - 1, lb_ref)
+        lane = lax.broadcasted_iota(jnp.int32, (1, 128), 1)
+        last = pl.ds(width - 128, 128)
+        v = jnp.where(lane == 127, m_ref[g], acc_ref[g, :, last])
+        acc_ref[g, :, last] = jnp.where(lane == 126, z_ref[g], v)
+
+    group(0, tp, True)
+    from_mate.wait_recv()
+    group(1, tp_m)
+    from_x.wait_recv()
+    relay.start()
+    back[0].start()
+    group(2, tp_x)
+    from_relay.wait_recv()
+    keep = pltpu.make_async_copy(fn_ref, fn_hbm, out_sem)
+    keep.start()
+    back[1].start()
+    group(3, tp_xm)
+    for b in back:
+        if b is back[2]:
+            b.start()
+        b.wait_recv()
+
+    def combine(i, _):
+        r = pl.ds(pl.multiple_of(i * 64, 64), 64)
+        last = pl.ds(width - 128, 128)
+        tails = [acc_ref[0, r, last]] + [got_ref[k, r, last] for k in range(3)]
+        peaks = [v[:, 127:128] for v in tails]
+        peak = jnp.maximum(jnp.maximum(peaks[0], peaks[1]), jnp.maximum(peaks[2], peaks[3]))
+        scales = [jnp.exp(p - peak) for p in peaks]
+        total = sum(v[:, 126:127] * s for v, s in zip(tails, scales))
+        lse_ref[r] = peak + jnp.log(total)
+        cols = pl.ds(0, d_stud)
+        num = acc_ref[0, r, cols] * scales[0]
+        for k in range(3):
+            num = num + got_ref[k, r, cols] * scales[k + 1]
+        dt_ref[r] = num / total
+        return 0
+
+    lax.fori_loop(0, rows // 64, combine, 0)
+    keep.wait()
+    for cp in (to_mate, to_x, relay, *back):
+        cp.wait_send()
+
+
+def head_stats(h_own, head_rows, head_cols, vocab_part, tp_size):
+    rows, d_model = h_own.shape
+    d_stud, padded = head_cols.shape
     chunk = head_chunk(vocab_part)
-    n_steps = pl.cdiv(vocab_part, chunk)
-    whole = lambda shape: pl.BlockSpec(shape, lambda i: (0, 0), pipeline_mode=pl.Buffered(1))
+    width = pl.cdiv(d_stud + 2, 128) * 128
+    any_spec = pl.BlockSpec(memory_space=pl.ANY)
+    vmem_spec = pl.BlockSpec(memory_space=pltpu.VMEM)
     return pl.pallas_call(
         functools.partial(stats_kernel, vocab_part),
         name='head_stats',
-        grid=(n_steps,),
-        out_shape=(jax.ShapeDtypeStruct((rows, 128), jnp.float32),
-                   jax.ShapeDtypeStruct((rows, d_stud), jnp.float32),
+        out_shape=(jax.ShapeDtypeStruct((tp_size, rows, d_model), jnp.bfloat16),
+                   jax.ShapeDtypeStruct((rows, 1), jnp.float32),
                    jax.ShapeDtypeStruct((rows, d_stud), jnp.float32)),
-        in_specs=[whole((rows, d_model)), whole((rows, d_stud)),
-                  pl.BlockSpec((d_model, chunk), lambda i: (0, i)),
-                  pl.BlockSpec((d_stud, chunk), lambda i: (0, i))],
-        out_specs=(whole((rows, 128)), whole((rows, d_stud)), whole((rows, d_stud))),
-        scratch_shapes=[pltpu.VMEM((rows, 1), jnp.float32)] * 5,
-        cost_estimate=pl.CostEstimate(flops=2 * rows * vocab_part * (d_model + 3 * d_stud),
+        in_specs=[vmem_spec, any_spec, vmem_spec],
+        out_specs=(any_spec, vmem_spec, vmem_spec),
+        scratch_shapes=[
+            pltpu.VMEM((tp_size, rows, d_model), jnp.bfloat16),
+            pltpu.VMEM((padded, d_model), jnp.bfloat16),
+            pltpu.VMEM((rows, chunk), jnp.float32),
+            pltpu.VMEM((rows, chunk), jnp.float32),
+            pltpu.VMEM((rows, chunk), jnp.bfloat16),
+            pltpu.VMEM((rows, 1), jnp.float32),
+            pltpu.VMEM((tp_size, rows, 1), jnp.float32),
+            pltpu.VMEM((tp_size, rows, 1), jnp.float32),
+            pltpu.VMEM((tp_size, rows, width), jnp.float32),
+            pltpu.VMEM((tp_size - 1, rows, width), jnp.float32),
+            pltpu.SemaphoreType.DMA((padded // chunk,)),
+            pltpu.SemaphoreType.DMA,
+            pltpu.SemaphoreType.DMA((6,)),
+            pltpu.SemaphoreType.DMA((6,)),
+        ],
+        compiler_params=pltpu.CompilerParams(collective_id=2, has_side_effects=True),
+        cost_estimate=pl.CostEstimate(flops=2 * tp_size * rows * vocab_part * (d_model + d_stud),
                                       bytes_accessed=2 * vocab_part * (d_model + d_stud),
-                                      transcendentals=2 * rows * vocab_part),
-    )(full_norm, stud_full, head_t, head_cols)
+                                      transcendentals=tp_size * rows * vocab_part),
+    )(h_own, head_rows, head_cols)
 
 
 HEAD_STAGES = 9
 
 
 def head_grad_kernel(vocab_part, n_chunks, kl_coef, fn_ref, s_ref, st_ref, lt_ref, ls_ref, wt_ref, ws_ref, out_ref,
-                     d_ref, part_ref, yb_ref, nb_ref, fb_ref, copy_sem, send_sem, recv_sem):
+                     d_ref, part_ref, yb_ref, nb_ref, fb_ref, kl_ref, copy_sem, send_sem, recv_sem):
     step = pl.program_id(0)
-    rows, chunk = fn_ref.shape[0], wt_ref.shape[1]
+    rows, chunk = fn_ref.shape[0], wt_ref.shape[0]
     d_stud = st_ref.shape[0]
     d_pad = part_ref.shape[1]
     half, quart, eighth = d_pad // 2, d_pad // 4, d_pad // 8
@@ -501,24 +679,31 @@
 
         def body(i, _):
             r = pl.ds(pl.multiple_of(i * blk, blk), blk)
-            lt = jnp.dot(fn_ref[r], wt_ref[...], preferred_element_type=jnp.float32)
+            lt = lax.dot_general(fn_ref[r], wt_ref[...], (((1,), (1,)), ((), ())), preferred_element_type=jnp.float32)
             ls = jnp.dot(s_ref[r], ws_ref[...], preferred_element_type=jnp.float32)
-            shift_t = jnp.concatenate([lt_ref[r]] * (chunk // 128), axis=1)
-            shift_s = jnp.concatenate([ls_ref[r]] * (chunk // 128), axis=1)
-            diff = kl_coef * (jnp.exp(ls - shift_s) - jnp.exp(lt - shift_t))
+            log_t = lt - jnp.concatenate([lt_ref[r]] * (chunk // 128), axis=1)
+            log_s = ls - jnp.concatenate([ls_ref[r]] * (chunk // 128), axis=1)
+            prob_t = jnp.exp(log_t)
+            diff = kl_coef * (jnp.exp(log_s) - prob_t)
+            kl = prob_t * (log_t - log_s)
             if masked:
                 diff = jnp.where(valid, diff, 0.0)
+                kl = jnp.where(valid, kl, 0.0)
             d_ref[r] = diff.astype(jnp.bfloat16)
+            kl = jnp.sum(kl.reshape(blk // 8, 8, chunk), axis=0)
+            kl_ref[...] += sum(kl[:, k * 128:(k + 1) * 128] for k in range(chunk // 128))
             return 0
 
         lax.fori_loop(0, rows // blk, body, 0)
         grad = jnp.dot(st_ref[...], d_ref[...], preferred_element_type=jnp.float32)
         part_ref[step, pl.ds(0, d_stud)] = grad
-        if d_pad > d_stud:
-            part_ref[step, pl.ds(d_stud, d_pad - d_stud)] = jnp.zeros((d_pad - d_stud, chunk), jnp.float32)
+        extra = pl.ds(d_stud, 8)
+        part_ref[step, extra] = jnp.zeros((8, chunk), jnp.float32)
+        part_ref[step, extra, pl.ds(0, 128)] = kl_ref[...]
 
     @pl.when(step == 0)
     def _():
+        kl_ref[...] = jnp.zeros_like(kl_ref)
         barrier = pltpu.get_barrier_semaphore()
         for dev in (x_peer, y_peer, near, far, mate):
             pl.semaphore_signal(barrier, inc=1, device_id=dev, device_id_type=MESH)
@@ -592,13 +777,13 @@
         lax.fori_loop(0, n_chunks, drain, 0)
 
 
-def head_grads(full_norm, stud_full, log_t, log_s, head_t, head_cols, kl_coef, tp_size):
+def head_grads(full_norm, stud_full, log_t, log_s, head_rows, head_cols, kl_coef, tp_size):
     rows, d_model = full_norm.shape
     d_stud = stud_full.shape[1]
-    vocab_part = head_t.shape[1]
-    chunk = head_chunk(vocab_part)
+    vocab_part = head_rows.shape[0]
+    chunk = grad_chunk(vocab_part)
     n_chunks = pl.cdiv(vocab_part, chunk)
-    d_pad = pl.cdiv(d_stud, 64) * 64
+    d_pad = pl.cdiv(d_stud + 8, 64) * 64
     whole = lambda shape: pl.BlockSpec(shape, lambda i: (0, 0), pipeline_mode=pl.Buffered(1))
     return pl.pallas_call(
         functools.partial(head_grad_kernel, vocab_part, n_chunks, kl_coef),
@@ -607,7 +792,7 @@
         out_shape=jax.ShapeDtypeStruct((tp_size, d_pad, n_chunks * chunk), jnp.float32),
         in_specs=[whole((rows, d_model)), whole((rows, d_stud)), whole((d_stud, rows)),
                   whole((rows, 128)), whole((rows, 128)),
-                  pl.BlockSpec((d_model, chunk), lambda i: (0, jnp.minimum(i, n_chunks - 1))),
+                  pl.BlockSpec((chunk, d_model), lambda i: (jnp.minimum(i, n_chunks - 1), 0)),
                   pl.BlockSpec((d_stud, chunk), lambda i: (0, jnp.minimum(i, n_chunks - 1)))],
         out_specs=pl.BlockSpec(memory_space=pl.ANY),
         scratch_shapes=[
@@ -616,6 +801,7 @@
             pltpu.VMEM((n_chunks, d_pad // 2, chunk), jnp.float32),
             pltpu.VMEM((n_chunks, d_pad // 4, chunk), jnp.float32),
             pltpu.VMEM((n_chunks, d_pad // 8, chunk), jnp.float32),
+            pltpu.VMEM((8, 128), jnp.float32),
             pltpu.SemaphoreType.DMA((n_chunks,)),
             pltpu.SemaphoreType.DMA((HEAD_STAGES, n_chunks)),
             pltpu.SemaphoreType.DMA((HEAD_STAGES, n_chunks)),
@@ -624,7 +810,7 @@
         cost_estimate=pl.CostEstimate(flops=200 * 10**9, bytes_accessed=2 * vocab_part * (d_model + d_stud),
                                       transcendentals=2 * rows * vocab_part),
     )(full_norm, stud_full, stud_full.T, jnp.broadcast_to(log_t[:, None], (rows, 128)),
-      jnp.broadcast_to(log_s[:, None], (rows, 128)), head_t, head_cols)
+      jnp.broadcast_to(log_s[:, None], (rows, 128)), head_rows, head_cols)
 
 
 def join_kernel(vocab_part, in_ref, out_ref):
@@ -652,48 +838,41 @@
 
     def local_step(x_teach, x_stud, w_up_t, w_down_t, gain_t, head_t, w_up_s, w_down_s, gain_s, proj_s, head_s):
         n_feat = w_up_s.shape[0]
-        feats = run_teacher(x_teach, w_up_t, w_down_t, gain_t, n_feat)
-        features = [feats[i].reshape(x_teach.shape) for i in range(n_feat)]
-        x_stud = lax.all_to_all(x_stud, 'tp', 1, 0, tiled=True)
-        final_norm = rms_parts(features[-1])[0].astype(jnp.bfloat16)
-        final_full = lax.all_gather(final_norm, 'tp', axis=0, tiled=True)
-        teach_logits = mat_mul('bsd,dv->bsv', final_full, head_t)
-
-        n_tokens = x_stud.shape[0] * x_stud.shape[1] * dp_size * tp_size
-        feat_coef = 1.0 / (n_feat * n_tokens * head_t.shape[0])
-        kl_coef = 1.0 / n_tokens
-        saved_acts, err_total = student_forward(x_stud, w_up_s, w_down_s, gain_s, proj_s, features)
         d_stud, d_teach = x_stud.shape[2], x_teach.shape[2]
         vocab_part = head_t.shape[1]
-        n_own = x_stud.shape[0] * x_stud.shape[1]
+        n_own = x_teach.shape[0] * x_teach.shape[1]
+        n_tokens = n_own * dp_size * tp_size
+        feat_coef = 1.0 / (n_feat * n_tokens * d_teach)
+        kl_coef = 1.0 / n_tokens
         tp_idx = lax.axis_index('tp')
-        head_in = saved_acts[-1][7]
-        stud_full = lax.all_gather(head_in, 'tp', axis=0, tiled=True).reshape(tp_size * n_own, d_stud)
-        full_norm = final_full.reshape(tp_size * n_own, d_teach)
+        x_stud = lax.all_to_all(x_stud, 'tp', 1, 0, tiled=True).reshape(1, n_own, d_stud)
+        saved_acts = student_forward(x_stud, w_up_s, w_down_s, gain_s)
+        head_in = saved_acts[-1][7].reshape(n_own, d_stud)
+        stud_full = lax.all_gather(head_in, 'tp', axis=0, tiled=True)
+        feats, lse_s, in_grad_s = run_teacher(x_teach, w_up_t, w_down_t, gain_t, n_feat, head_in, head_s)
         head_cols = lax.dynamic_slice_in_dim(head_s, tp_idx * vocab_part, vocab_part, axis=1)
-        stats, acc_t, acc_s = head_stats(full_norm, stud_full, head_t, head_cols)
-        all_stats = lax.all_gather(stats[:, :5].T, 'tp', axis=0)
-        peaks = jnp.max(all_stats[:, 0::2][:, :2], axis=0)
-        scales = jnp.exp(all_stats[:, 0:4:2] - peaks)
-        sums = jnp.sum(all_stats[:, 1:4:2] * scales, axis=0)
-        log_norms = peaks + jnp.log(sums)
-        kl_tokens = (jnp.sum(all_stats[:, 4] * scales[:, 0], axis=0) / sums[0]) - (log_norms[0] - log_norms[1])
-        kl_local = jnp.sum(lax.dynamic_slice_in_dim(kl_tokens, tp_idx * n_own, n_own))
-        own_t = jnp.exp(stats[:, 0] - log_norms[0])[:, None]
-        own_s = jnp.exp(stats[:, 2] - log_norms[1])[:, None]
-        full_in_grad = kl_coef * (acc_s * own_s - acc_t * own_t)
-        head_in_grad = lax.psum_scatter(full_in_grad, 'tp', scatter_dimension=0, tiled=True).reshape(x_stud.shape)
-        grad_up, grad_down, grad_gain, grad_proj = student_backward(
-            saved_acts, w_up_s, w_down_s, gain_s, proj_s, feat_coef, head_in_grad)
-        loss_part = feat_coef * err_total + kl_coef * kl_local
-        extra = jnp.stack([grad_gain, jnp.full_like(grad_gain, loss_part)], axis=-1)
-        packed = jnp.concatenate([grad_proj, extra], axis=-1)
-        log_norms, grad_up, grad_down, packed = lax.optimization_barrier((log_norms, grad_up, grad_down, packed))
-        grad_up, grad_down, packed = lax.psum((grad_up, grad_down, packed), ('dp', 'tp'))
-        parts = head_grads(full_norm, stud_full, log_norms[0], log_norms[1], head_t, head_cols, kl_coef, tp_size)
+        padded = pl.cdiv(vocab_part, head_chunk(vocab_part)) * head_chunk(vocab_part)
+        head_cols = jnp.pad(head_cols, ((0, 0), (0, padded - vocab_part)))
+        head_rows = head_t.T
+        err_grads, err_total, grad_proj = student_errors(saved_acts, proj_s, feats[:, None], feat_coef)
+        h_own, grad_proj, stud_full = lax.optimization_barrier((feats[-1], grad_proj, stud_full))
+        grad_proj = lax.psum(grad_proj, ('dp', 'tp'))
+        full_norm, lse_t, in_grad_t = head_stats(h_own, head_rows, head_cols, vocab_part, tp_size)
+        log_norms = lax.all_gather(jnp.concatenate([lse_t, lse_s], axis=1).T, 'tp', axis=0)
+        head_in_grad = (kl_coef * (in_grad_s - in_grad_t)).reshape(x_stud.shape)
+        grad_up, grad_down, grad_gain = student_backward(saved_acts, w_up_s, w_down_s, gain_s, proj_s, err_grads, head_in_grad)
+        extra = jnp.stack([grad_gain, jnp.full_like(grad_gain, feat_coef * err_total)], axis=-1)
+        grad_up = jnp.concatenate([grad_up, extra], axis=-1)
+        log_norms, grad_up, grad_down, grad_proj = lax.optimization_barrier((log_norms, grad_up, grad_down, grad_proj))
+        grad_up, grad_down = lax.psum((grad_up, grad_down), ('dp', 'tp'))
+        log_t, log_s = log_norms[:, 0].reshape(-1), log_norms[:, 1].reshape(-1)
+        parts = head_grads(full_norm.reshape(-1, d_teach), stud_full, log_t, log_s, head_rows, head_cols, kl_coef, tp_size)
         head_grad = join_quarters(parts, d_stud, vocab_part)
-        grad_proj, grad_gain = packed[..., :d_teach], packed[..., d_teach]
-        total_loss = packed[0, 0, d_teach + 1]
+        last = (pl.cdiv(vocab_part, grad_chunk(vocab_part)) - 1) * grad_chunk(vocab_part)
+        kl_sum = jnp.sum(parts[:, d_stud:d_stud + 8, last:last + 128])
+        d_ff = w_up_s.shape[2]
+        total_loss = grad_up[0, 0, d_ff + 1] + kl_coef * kl_sum
+        grad_up, grad_gain = grad_up[..., :d_ff], grad_up[..., d_ff]
         return total_loss, grad_up, grad_down, grad_gain, grad_proj, head_grad
 
     in_specs = (P('dp', 'tp', None), P(('dp', 'tp'), None, None), P(None, None, 'tp'), P(None, 'tp', None),

time: 1050 us -> 1020 us (0.971)
  waiting for transfers between devices: 28.7 us -> 115 us
  Pallas kernels: 866 us -> 783 us
  local copies, waits for them, and re-layouts: 62.6 us -> 43.9 us
  other arithmetic: 26.1 us -> 8.04 us
    psum x1 -> x2, waiting for transfers between devices: 0.01 us -> 114 us  [the longest x1 114 us: local_step(): grad_proj = lax.psum(grad_proj, ('dp', 'tp'))]
    pallas_call x1, Pallas kernels: 158 us -> 92.7 us  [head_stats(): pl.pallas_call(functools.partial(stats_kernel, vocab_part), name='head_st...]
    pallas_call x1, Pallas kernels: 343 us -> 312 us  [head_grads(): pl.pallas_call(functools.partial(head_grad_kernel, vocab_part, n_chunks,...]
    unnamed x88 -> x46, local copies, waits for them, and re-layouts: 37.3 us -> 13.7 us
    reduce_scatter x1 -> x0, waiting for transfers between devices: 14.3 us -> none  [local_step(): lax.psum_scatter(full_in_grad, 'tp', scatter_dimension=0, tiled=True)]
    pallas_call x1, Pallas kernels: 333 us -> 346 us  [run_teacher(): pl.pallas_call(functools.partial(teacher_kernel, n_layers), name='teacher...]
  transfers between devices with their start and end apart: 5 -> 4, of which waited for: 3 -> 2; matrix products, arithmetic and copies ran while one was open for 5% -> 5% of each run, Pallas kernels for 68% -> 68%
where the time goes in v3:
time: 1020 us; the launch traced here: 1010 us
  Pallas kernels  783 us (77%)
  waiting for transfers between devices  115 us (11%)
  local copies, waits for them, and re-layouts  43.9 us (4%)
  matrix products  31.7 us (3%)
  between operations  18.1 us (2%)
    pallas_call x1, Pallas kernels, run_teacher(): pl.pallas_call(functools.partial(teacher_kernel, n_layers), name='teacher...  346 us
    pallas_call x1, Pallas kernels, head_grads(): pl.pallas_call(functools.partial(head_grad_kernel, vocab_part, n_chunks,...  312 us
    psum x1, waiting for transfers between devices, local_step(): grad_proj = lax.psum(grad_proj, ('dp', 'tp'))  114 us
    pallas_call x1, Pallas kernels, head_stats(): pl.pallas_call(functools.partial(stats_kernel, vocab_part), name='head_st...  92.7 us
    pallas_call x1, Pallas kernels, join_quarters(): pl.pallas_call(functools.partial(join_kernel, vocab_part), name='join_qua...  32 us
    dot_general x18, matrix products, mat_mul(): jnp.einsum(subscripts, lhs_arr, rhs_arr, preferred_element_type=jnp.float32)  31.7 us
  transfers between devices with their start and end apart: 4, of which 2 were waited for; matrix products, arithmetic and copies ran while one was open for 5% of the time, Pallas kernels for 68%

profile of v3, /device:TPU:0, one launch (start us, length us, event | category | flops | bytes accessed | tf_op | source)
XLA Modules:
  0.0 1009.5 jit_solution(13933423971349268418)
XLA Ops:
  7.2 1.9 copy.43
  9.1 4.2 all-to-all-start
  13.3 4.1 constant_dynamic-slice_fusion
  17.5 2.5 pad.4.ws_ref
  28.8 345.8 %teacher.1 = (bf16[2,512,1024]{2,1,0:T(8,128)(2,1)}, f32[512,1]{1,0:T(8,128)}, f32[512,312]{1,0:T(8,128)}, bf16[3,8,1024,1024]{3,2,1,0:T(8,128)(2,1)}, bf16[3,8,1024,1024]{3,2,1,0:T(8,128)(2,1)}) custom-call(bf16[512,1024]{1,0:T(8,128)(2,1)} %bitcast.107, f32[8,1024]{1,0:T(8,128)} %gain_ref.1, bf16[512,312]{1,0:T(8,128)(2,1)} %copy.48.s_ref, ...), custom_call_target="tpu_custom_call" | custom-call | flops 68719476736 | bytes 134217728 | tf_op jit(solution)/shard_map/teacher/pallas_call | solution.py:368
  374.6 2.2 copy.53
  378.0 3.1 multiply_reduce_fusion
  381.1 4.1 multiply_reduce_fusion.1
  390.4 2.4 slice_bitcast_fusion.h_ref
  392.8 2.5 fusion.36
  395.3 92.7 %head_stats.1 = (bf16[4,512,1024]{2,1,0:T(8,128)(2,1)}, f32[512,1]{1,0:T(8,128)}, f32[512,312]{1,0:T(8,128)}) custom-call(bf16[512,1024]{1,0:T(8,128)(2,1)} %slice_bitcast_fusion.h_ref, bf16[7648,1024]{1,0:T(8,128)(2,1)} %bitcast.105, bf16[312,7680]{1,0:T(8,128)(2,1)} %pad.4.ws_ref), custom_call_target="tpu_custom_call" | custom-call | flops 41851813888 | bytes 20435456 | tf_op jit(solution)/shard_map/head_stats/pallas_call | solution.py:565
  488.0 2.2 copy.54
  490.2 2.2 multiply_reduce_fusion.6
  492.9 2.3 fusion.13
  497.7 2.3 fusion.6
  504.4 2.1 pad_maximum_fusion
  507.7 2.5 copy.56.s_ref
  511.0 4.0 concatenate.7
  515.0 5.5 all-gather.1
  520.5 3.0 convolution_bitcast_fusion.1
  526.6 113.8 %all-reduce.5.cloned.1.call-done = f32[2,312,1024]{2,1,0:T(8,128)} async-done(((f32[2,312,1024]{2,1,0:T(8,128)}), f32[2,312,1024]{2,1,0:T(8,128)}) %all-reduce.5.cloned.1.call-update) | async-done | bytes 2555920 | tf_op jit(solution)/shard_map/psum | solution.py:859
  643.1 312.4 %head_grads.1.in_ref = f32[4,320,7680]{2,1,0:T(8,128)} custom-call(bf16[2048,1024]{1,0:T(8,128)(2,1)} %bitcast.108, bf16[2048,312]{1,0:T(8,128)(2,1)} %copy.56.s_ref, bf16[312,2048]{1,0:T(8,128)(2,1)} %bitcast.102, f32[2048,128]{1,0:T(8,128)} %broadcast_in_dim.9.lt_ref, f32[2048,128]{1,0:T(8,128)} %broadcast_in_dim.11.ls_ref, bf16[7648,1024]{1,0:T(8,128)(2,1)} %bitcast.106, ...), custom_call_target="tpu_custom_call" | custom-call | flops 199999995904 | bytes 20435456 | tf_op jit(solution)/shard_map/head_grads/pallas_call | solution.py:788
  957.5 32.0 %join_quarters.1 = f32[312,30592]{1,0:T(8,128)} custom-call(f32[4,320,7680]{2,1,0:T(8,128)} %head_grads.1.in_ref), custom_call_target="tpu_custom_call" | custom-call | flops 9544704 | bytes 76357632 | tf_op jit(solution)/shard_map/join_quarters/pallas_call | solution.py:823
  993.2 3.9 copy.63
  (98 shorter events, 37.5 us)
Async XLA Ops:
  9.1 11.6 %all-to-all-start = ((bf16[2,256,312]{2,0,1:T(2,128)(2,1)}), bf16[2,256,312]{2,0,1:T(2,128)(2,1)S(1)}, u32[]{:S(2)}, u32[]{:S(2)}) async-start(bf16[2,256,312]{2,0,1:T(2,128)(2,1)} %copy.43), calls=%async_computation | async-start | bytes 786432 | tf_op jit(solution)/shard_map/all_to_all | solution.py:848
  13.3 382.0 %all-gather.4.cloned.1.call-start = ((), (), s32[]{:S(2)}) async-start(), calls=%async_computation.1 | async-start | bytes 1597440 | tf_op jit(solution)/shard_map/all_gather | solution.py:851
  17.5 2.5 copy-start.18
  20.8 1.4 copy-start.13
  21.6 2.9 copy-start.6
  21.6 1.8 copy-start.19
  23.3 1.5 copy-start.8
  25.7 1.5 copy-start.10
  28.2 612.2 %all-reduce.5.cloned.1.call-start = ((), (), s32[]{:S(2)}) async-start(), calls=%async_computation.2 | async-start | bytes 5111808 | tf_op jit(solution)/shard_map/psum | solution.py:859
  386.5 1.7 copy-start
  390.4 2.4 copy-start.1
  490.2 2.4 copy-start.11
  490.2 2.8 copy-start.20
  492.9 2.3 copy-start.15
  492.9 2.3 copy-start.4
  492.9 2.3 copy-start.14
  496.0 1.7 copy-start.9
  497.7 2.3 copy-start.17
  497.7 2.3 copy-start.7
  504.3 485.2 %all-reduce.7.cloned.1.call-start = ((), (), s32[]{:S(2)}) async-start(), calls=%async_computation.3 | async-start | bytes 12779520 | tf_op jit(solution)/shard_map/psum | solution.py:867
  520.5 3.1 copy-start.12
  520.5 3.1 copy-start.16
  993.2 4.0 copy-start.3
  997.2 2.9 copy-start.5
  (1 other events, 0.9 us)
Sparse Core Ops, SparseCore 0:
  28.4 26.6 all-gather.3
  504.4 135.9 all-reduce.4
  646.9 219.3 all-reduce.6
